TPU v7x, 16 devices: a whole 2x2x2 slice. The times are simulated.
16 devices in a mesh: fsdp: 4 (over z, y), ep: 4 (over x, core).
Axes of the slice: x: 2, y: 2, z: 2, core: 2. Of those that a mesh axis runs over, the one named last changes fastest.
Arguments:
- x_in: bfloat16 [2, 16384, 896], P(None, ('fsdp', 'ep'))
- dy_out: bfloat16 [2, 16384, 896], P(None, ('fsdp', 'ep'))
- expert_idx: int32 [2, 16384, 8], P(None, ('fsdp', 'ep'))
- gate_prob: float32 [2, 16384, 8], P(None, ('fsdp', 'ep'))
- w_one: bfloat16 [64, 896, 640], P('ep', 'fsdp')
- w_two: bfloat16 [64, 640, 896], P('ep', None, 'fsdp')
- w_three: bfloat16 [64, 896, 640], P('ep', 'fsdp')
Outputs:
- output 1: bfloat16 [2, 16384, 896], P(None, ('fsdp', 'ep'))
- output 2: float32 [2, 16384, 8], P(None, ('fsdp', 'ep'))
- output 3: float32 [64, 896, 640], P('ep', 'fsdp')
- output 4: float32 [64, 640, 896], P('ep', None, 'fsdp')
- output 5: float32 [64, 896, 640], P('ep', 'fsdp')
All inputs are finite; a program needn't handle non-finite values.
Results may differ from a plain program's by a relative error of at most 0.0011.
Values are sent between devices in bfloat16 or wider.
A program may use at most 1 GiB of HBM per device.

v0:
```python
import functools

import jax
import jax.numpy as jnp
from jax import lax
from jax.experimental import pallas as pl
from jax.experimental.pallas import tpu as pltpu
from jax.sharding import Mesh, PartitionSpec as P


MICRO = 2
TOK = 1024
TOP_K = 8
D = 896
F = 640
CAP = 160
SRC = 8
EXP = 8
QUARTER = D // 4
HALF = D // 2
ROWS = SRC * CAP
CHUNKS = (1, 2, 2, 2, 1)
STARTS = (0, 1, 3, 5, 7)
GRAIN = 16
TILE = 256
N_CHUNK = len(CHUNKS)
WIDE = 3 * F
SUM_ROWS = TOK + 16
TABLE_ROWS = 64

BF16 = jnp.bfloat16
F32 = jnp.float32
VMEM_LIMIT = 62 * 1024 * 1024


def params(**kw):
    return pltpu.CompilerParams(vmem_limit_bytes=VMEM_LIMIT, **kw)


PIECES = 4


def token_kernel(mb, x_ref, dy_ref, ids_ref, gate_ref, out_ref, buf, table, in_sem, out_sem):
    rows = TOK // PIECES
    loads = []
    for half, src in enumerate((x_ref, dy_ref)):
        for i in range(PIECES):
            place = pl.ds((half * PIECES + i) * rows, rows)
            loads.append(pltpu.make_async_copy(src.at[mb, pl.ds(i * rows, rows), :], buf.at[place, :], in_sem.at[half * PIECES + i]))
    for load in loads:
        load.start()
    gate = gate_ref[mb]
    high = gate.astype(BF16).astype(F32)
    mid = (gate - high).astype(BF16).astype(F32)
    low = gate - high - mid
    rows_f = jnp.concatenate([ids_ref[mb].astype(F32), high, mid, low], axis=0)
    table[:32, :] = rows_f[:, :D].astype(BF16)
    table[32:, :] = jnp.zeros((32, D), BF16)
    table[32:, :TOK - D] = rows_f[:, D:].astype(BF16)
    stores = []
    for i, load in enumerate(loads):
        load.wait()
        place = pl.ds(i * rows, rows)
        stores.append(pltpu.make_async_copy(buf.at[place, :], out_ref.at[place, :], out_sem))
        stores[-1].start()
    stores.append(pltpu.make_async_copy(table, out_ref.at[pl.ds(2 * TOK, TABLE_ROWS), :], out_sem))
    stores[-1].start()
    for store in stores:
        store.wait()


def token_block(x_in, dy_out, ids, gate, mb):
    anywhere = pl.BlockSpec(memory_space=pl.ANY)
    return pl.pallas_call(
        functools.partial(token_kernel, mb),
        out_shape=jax.ShapeDtypeStruct((2 * TOK + TABLE_ROWS, D), BF16),
        in_specs=[anywhere, anywhere, pl.BlockSpec(memory_space=pltpu.VMEM), pl.BlockSpec(memory_space=pltpu.VMEM)],
        out_specs=anywhere,
        scratch_shapes=[
            pltpu.VMEM((2 * TOK, D), BF16),
            pltpu.VMEM((TABLE_ROWS, D), BF16),
            pltpu.SemaphoreType.DMA((2 * PIECES,)),
            pltpu.SemaphoreType.DMA,
        ],
        compiler_params=params(),
        name="token_block",
        cost_estimate=pl.CostEstimate(flops=1 << 20, bytes_accessed=8 << 20, transcendentals=0),
    )(x_in, dy_out, ids, gate)


def routing_kernel(first_ref, *refs):
    tables = refs[:SRC]
    pos_ref, gsel_ref, ids_ref, cnt_ref, member = refs[SRC:]
    first = first_ref[0]
    for src in range(SRC):
        block = tables[src][...].astype(F32)
        table = jnp.concatenate([block[:32], block[32:, :TOK - D]], axis=1)
        ids = table[:8].astype(jnp.int32)
        gate = table[8:16] + table[16:24] + table[24:]
        ids_ref[src] = ids
        for e in range(EXP):
            hit = ids == first + e
            row = src * EXP + e
            member[row:row + 1, :] = jnp.sum(jnp.where(hit, 1.0, 0.0), axis=0, keepdims=True)
            gsel_ref[src, e:e + 1, :] = jnp.sum(jnp.where(hit, gate, 0.0), axis=0, keepdims=True)
    earlier = lax.broadcasted_iota(jnp.int32, (TOK, TOK), 0) < lax.broadcasted_iota(jnp.int32, (TOK, TOK), 1)
    chosen = member[...]
    count = jnp.dot(chosen.astype(BF16), jnp.where(earlier, 1.0, 0.0).astype(BF16), preferred_element_type=F32)
    kept = (chosen > 0.5) & (count < CAP - 0.5)
    slot = jnp.where(kept, count, -1.0).astype(jnp.int32)
    pos_ref[...] = slot.reshape(SRC, EXP, TOK)
    load = lax.dot_general(jnp.ones((8, TOK), BF16), chosen.astype(BF16), (((1,), (1,)), ((), ())), preferred_element_type=F32)
    rows = jnp.minimum(load, float(CAP)).astype(jnp.int32)
    cnt_ref[...] = ((rows + (GRAIN - 1)) >> 4) << 4


def routing(first, tokens):
    shape = (SRC, EXP, TOK)
    table = pl.BlockSpec((TABLE_ROWS, D), lambda i: (2 * TOK // TABLE_ROWS, 0))
    whole = pl.BlockSpec(shape, lambda i: (0, 0, 0))
    return pl.pallas_call(
        routing_kernel,
        grid=(1,),
        out_shape=(jax.ShapeDtypeStruct(shape, jnp.int32), jax.ShapeDtypeStruct(shape, F32), jax.ShapeDtypeStruct(shape, jnp.int32), jax.ShapeDtypeStruct((8, SRC * EXP), jnp.int32)),
        in_specs=[pl.BlockSpec(memory_space=pltpu.SMEM)] + [table] * SRC,
        out_specs=(whole, whole, whole, pl.BlockSpec((8, SRC * EXP), lambda i: (0, 0))),
        scratch_shapes=[pltpu.VMEM((SRC * EXP, TOK), F32)],
        compiler_params=params(),
        name="routing",
        cost_estimate=pl.CostEstimate(flops=2 * 64 * TOK * TOK, bytes_accessed=3 << 20, transcendentals=0),
    )(first, *tokens)


def aligned(value):
    return pl.multiple_of(value, GRAIN)


def gather_kernel(lo, n, cnt_ref, *refs):
    tok_refs = refs[:SRC]
    pos_ref, gate_ref = refs[SRC:SRC + 2]
    out_refs = refs[SRC + 2:SRC + 5]
    pick, gcol, buf, stage, offset, sem, out_sem = refs[SRC + 5:]
    s = pl.program_id(0)
    slot = lax.rem(s, 2)

    def fetch(src):
        return pltpu.make_async_copy(tok_refs[src].at[pl.ds(0, 2 * TOK), :], buf.at[src % 2], sem.at[src % 2])

    def store(which, j, side, start, place):
        return pltpu.make_async_copy(
            stage.at[side, which, pl.ds(aligned(start), CAP), :], out_refs[which].at[j, pl.ds(aligned(place), CAP), :], out_sem.at[side]
        )

    @pl.when(s == 0)
    def _():
        fetch(0).start()
        for j in range(n):
            offset[j] = 0

    for src in range(1, SRC):
        @pl.when(s == src - 1)
        def _(src=src):
            fetch(src).start()

    slots = lax.broadcasted_iota(jnp.int32, (CAP, TOK), 0)
    starts = []
    total = jnp.int32(0)
    for j in range(n):
        e = lo + j
        rows = pl.ds(aligned(total), CAP)
        hit = slots == pos_ref[e:e + 1, :]
        pick[rows, :] = jnp.where(hit, 1.0, 0.0).astype(BF16)
        col = jnp.sum(jnp.where(hit, gate_ref[e:e + 1, :], 0.0), axis=1, keepdims=True)
        gcol[rows, :] = jnp.broadcast_to(col, (CAP, 128))
        starts.append(total)
        total = total + cnt_ref[0, s * EXP + e]

    for src in range(SRC):
        @pl.when(s == src)
        def _(src=src):
            fetch(src).wait()

    def body(t, carry):
        rows = pl.ds(pl.multiple_of(t * TILE, TILE), TILE)
        sel = pick[rows, :]
        x_rows = jnp.dot(sel, buf[slot, :TOK, :], preferred_element_type=F32)
        stage[slot, 0, rows, :] = x_rows.astype(BF16)
        dy_rows = jnp.dot(sel, buf[slot, TOK:, :], preferred_element_type=F32)
        stage[slot, 1, rows, :] = dy_rows.astype(BF16)
        stage[slot, 2, rows, :] = (gcol[rows, :1] * dy_rows).astype(BF16)
        return carry

    lax.fori_loop(0, (total + (TILE - 1)) // TILE, body, 0)

    @pl.when(s > 0)
    def _():
        for j in range(n):
            for which in range(3):
                store(which, j, 1 - slot, 0, 0).wait()

    for j in range(n):
        place = offset[j]
        for which in range(3):
            store(which, j, slot, starts[j], place).start()
        offset[j] = place + cnt_ref[0, s * EXP + lo + j]

    @pl.when(s == SRC - 1)
    def _():
        for j in range(n):
            for which in range(3):
                store(which, j, slot, 0, 0).wait()


def gather_rows(counts, tokens, pos, gate, lo, n):
    rows = jax.ShapeDtypeStruct((n, ROWS, D), BF16)
    table = pl.BlockSpec((None, EXP, TOK), lambda s: (s, 0, 0))
    anywhere = pl.BlockSpec(memory_space=pl.ANY)
    picked = (n * CAP + TILE - 1) // TILE * TILE
    return pl.pallas_call(
        functools.partial(gather_kernel, lo, n),
        grid=(SRC,),
        out_shape=(rows, rows, rows),
        in_specs=[pl.BlockSpec(memory_space=pltpu.SMEM)] + [anywhere] * SRC + [table, table],
        out_specs=(anywhere, anywhere, anywhere),
        scratch_shapes=[
            pltpu.VMEM((picked, TOK), BF16),
            pltpu.VMEM((picked, 128), F32),
            pltpu.VMEM((2, 2 * TOK, D), BF16),
            pltpu.VMEM((2, 3, picked, D), BF16),
            pltpu.SMEM((n,), jnp.int32),
            pltpu.SemaphoreType.DMA((2,)),
            pltpu.SemaphoreType.DMA((2,)),
        ],
        compiler_params=params(),
        name="gather_rows",
        cost_estimate=pl.CostEstimate(flops=4 * SRC * n * CAP * TOK * D, bytes_accessed=(30 + 7 * n) << 20, transcendentals=0),
    )(counts, *tokens, pos, gate)


def expert_kernel(add_into, lo, n, place_ref, cnt_ref, x_ref, dy_ref, g_ref, own_ref, yr_ref, zo_ref, zf_ref, *refs):
    if add_into:
        acc_ref, dx_ref, dg_ref, keep_ref, send_ref = refs[:5]
        refs = refs[5:]
    else:
        dx_ref, dg_ref, part_ref = refs[:3]
        refs = refs[3:]
    w, dws, w_sem, acc_sem, out_sem = refs
    i = pl.program_id(0)
    side = lax.rem(i, 2)
    dw = dws.at[side]
    z, y = place_ref[0], place_ref[1]
    quarters = (2 * z + y, 2 * z + 1 - y, 2 * (1 - z) + y, 2 * (1 - z) + 1 - y)

    def weight_copies(j):
        return [
            pltpu.make_async_copy(ref.at[j], w.at[j, pl.ds(pl.multiple_of(q * QUARTER, QUARTER), QUARTER), :], w_sem.at[j])
            for ref, q in zip((own_ref, yr_ref, zo_ref, zf_ref), quarters)
        ]

    def acc_copy(j):
        return pltpu.make_async_copy(acc_ref.at[j], dws.at[lax.rem(j, 2)], acc_sem)

    def out_copies(j):
        total = dws.at[lax.rem(j, 2)]
        if not add_into:
            return [pltpu.make_async_copy(total, part_ref.at[j], out_sem.at[0])]
        return [
            pltpu.make_async_copy(total.at[pl.ds(pl.multiple_of(z * HALF, HALF), HALF), :], keep_ref.at[j], out_sem.at[0]),
            pltpu.make_async_copy(total.at[pl.ds(pl.multiple_of((1 - z) * HALF, HALF), HALF), :], send_ref.at[j], out_sem.at[1]),
        ]

    @pl.when(i == 0)
    def _():
        for j in range(n):
            for copy in weight_copies(j):
                copy.start()
        if add_into:
            acc_copy(0).start()

    count = cnt_ref[0, lo + i]
    for src in range(1, SRC):
        count = count + cnt_ref[0, src * EXP + lo + i]

    if not add_into:
        dw[...] = jnp.zeros((D, WIDE), F32)
    for copy in weight_copies(i):
        copy.wait()
    if add_into:
        acc_copy(i).wait()

    def tile(start, size):
        rows = pl.ds(pl.multiple_of(start, TILE), size)
        live = lax.broadcasted_iota(jnp.int32, (size, 1), 0) < count - start
        x_c = jnp.where(live, x_ref[rows, :].astype(F32), 0.0).astype(BF16)
        g_c = jnp.where(live, g_ref[rows, :].astype(F32), 0.0).astype(BF16)
        h = jnp.dot(x_c, w[i, :, :2 * F], preferred_element_type=F32)
        h_one = h[:, :F]
        h_three = h[:, F:]
        sigma = jax.nn.sigmoid(h_one)
        silu = h_one * sigma
        act = (silu * h_three).astype(BF16)
        back = jnp.dot(dy_ref[rows, :], w[i, :, 2 * F:], preferred_element_type=F32)
        dg = jnp.sum(act.astype(F32) * back, axis=1, keepdims=True)
        dg_ref[rows, :] = jnp.broadcast_to(dg, (size, 128))
        d_act = jnp.dot(g_c, w[i, :, 2 * F:], preferred_element_type=F32)
        dh_three = (d_act * silu).astype(BF16)
        dh_one = (d_act * h_three * sigma * (1.0 + h_one * (1.0 - sigma))).astype(BF16)
        dh = jnp.concatenate([dh_one, dh_three], axis=1)
        dx = lax.dot_general(dh, w[i, :, :2 * F], (((1,), (1,)), ((), ())), preferred_element_type=F32)
        dx_ref[rows, :] = dx.astype(BF16)
        dw[:, :2 * F] += jnp.dot(x_c.T, dh, preferred_element_type=F32)
        dw[:, 2 * F:] += jnp.dot(g_c.T, act, preferred_element_type=F32)

    pairs = (count + (TILE - 1)) // (2 * TILE)

    def body(t, carry):
        tile(t * (2 * TILE), 2 * TILE)
        return carry

    lax.fori_loop(0, pairs, body, 0)

    @pl.when(pairs * (2 * TILE) < count)
    def _():
        tile(pairs * (2 * TILE), TILE)

    @pl.when(i > 0)
    def _():
        for copy in out_copies(i - 1):
            copy.wait()

    for copy in out_copies(i):
        copy.start()
    if add_into:
        @pl.when(i + 1 < n)
        def _():
            acc_copy(i + 1).start()

    @pl.when(i == n - 1)
    def _():
        for copy in out_copies(i):
            copy.wait()


def run_experts(place, counts, rows, offset, pieces, acc, k):
    add_into = acc is not None
    n = CHUNKS[k]
    row_in = pl.BlockSpec((None, ROWS, D), lambda i: (offset + i, 0, 0))
    anywhere = pl.BlockSpec(memory_space=pl.ANY)
    dx_out = pl.BlockSpec((None, ROWS, D), lambda i: (i, 0, 0))
    dg_out = pl.BlockSpec((None, ROWS, 128), lambda i: (i, 0, 0))
    outs = [jax.ShapeDtypeStruct((n, ROWS, D), BF16), jax.ShapeDtypeStruct((n, ROWS, 128), F32)]
    out_specs = [dx_out, dg_out]
    if add_into:
        outs += [jax.ShapeDtypeStruct((n, HALF, WIDE), F32)] * 2
        out_specs += [anywhere, anywhere]
    else:
        outs += [jax.ShapeDtypeStruct((n, D, WIDE), F32)]
        out_specs += [anywhere]
    operands = [place, counts, *rows, *pieces] + ([acc] if add_into else [])
    smem = pl.BlockSpec(memory_space=pltpu.SMEM)
    return pl.pallas_call(
        functools.partial(expert_kernel, add_into, STARTS[k], n),
        grid=(n,),
        out_shape=tuple(outs),
        in_specs=[smem, smem] + [row_in] * 3 + [anywhere] * (4 + add_into),
        out_specs=tuple(out_specs),
        scratch_shapes=[
            pltpu.VMEM((n, D, WIDE), BF16),
            pltpu.VMEM((2, D, WIDE), F32),
            pltpu.SemaphoreType.DMA((n,)),
            pltpu.SemaphoreType.DMA,
            pltpu.SemaphoreType.DMA((2,)),
        ],
        compiler_params=params(),
        name="experts_second" if add_into else "experts_first",
        cost_estimate=pl.CostEstimate(flops=n * 18 * ROWS * D * F, bytes_accessed=n * (24 << 20), transcendentals=n * 2 * ROWS * F),
    )(*operands)


def combine_kernel(base, steps, extras, final, first_ref, cnt_ref, *refs):
    dx_refs = refs[:N_CHUNK]
    dg_refs = refs[N_CHUNK:2 * N_CHUNK]
    refs = refs[2 * N_CHUNK:]
    pos_ref, ids_ref = refs[:2]
    extra_refs = refs[2:2 + extras]
    refs = refs[2 + extras:]
    if final == 2:
        refs = refs[2:]
    if final:
        dx_out, dg_out, sums = refs[:3]
        refs = refs[3:]
    else:
        sums = refs[0]
        refs = refs[1:]
    pick, rows, stage, dg_stage, sem = refs
    step = pl.program_id(0)
    side = lax.rem(step, 2)
    first = first_ref[0]

    def loads(i):
        source = base + 2 * i
        out = []
        for k in range(N_CHUNK):
            for j in range(CHUNKS[k]):
                e = STARTS[k] + j
                place = jnp.int32(0)
                for src in range(SRC - 1):
                    place = place + jnp.where(src < source, cnt_ref[0, src * EXP + e], 0)
                window = pl.ds(aligned(place), CAP)
                out.append(pltpu.make_async_copy(dx_refs[k].at[j, window, :], stage.at[lax.rem(i, 2), e], sem.at[lax.rem(i, 2)]))
                out.append(pltpu.make_async_copy(dg_refs[k].at[j, window, :], dg_stage.at[lax.rem(i, 2), e], sem.at[lax.rem(i, 2)]))
        return out

    @pl.when(step == 0)
    def _():
        for load in loads(step):
            load.start()
        rows[...] = jnp.zeros((ROWS + TILE, D), BF16)

    @pl.when(step + 1 < steps)
    def _():
        for load in loads(step + 1):
            load.start()

    source = base + 2 * step
    slots = lax.broadcasted_iota(jnp.int32, (CAP, TOK), 0)
    total = jnp.int32(0)
    starts, counts = [], []
    for e in range(EXP):
        pick[pl.ds(aligned(total), CAP), :] = jnp.where(slots == pos_ref[e:e + 1, :], 1.0, 0.0).astype(BF16)
        starts.append(total)
        counts.append(cnt_ref[0, source * EXP + e])
        total = total + counts[e]
    pick[pl.ds(aligned(total), TILE), :] = jnp.zeros((TILE, TOK), BF16)

    for load in loads(step):
        load.wait()
    ids = ids_ref[...]
    dg_choice = jnp.zeros((TOP_K, TOK), F32)
    for e in range(EXP):
        block = stage[side, e]
        if e == EXP - 1:
            live = lax.broadcasted_iota(jnp.int32, (CAP, 1), 0) < counts[e]
            block = jnp.where(live, block.astype(F32), 0.0).astype(BF16)
        rows[pl.ds(aligned(starts[e]), CAP), :] = block
        hit = slots == pos_ref[e:e + 1, :]
        dg_tok = jnp.sum(jnp.where(hit, dg_stage[side, e, :, :1], 0.0), axis=0, keepdims=True)
        dg_choice = dg_choice + jnp.where(ids == first + e, dg_tok, 0.0)

    start = jnp.zeros((TOK, D), F32)
    left = dg_choice[:, :D]
    right = dg_choice[:, D:]
    for extra in extra_refs:
        start = start + extra[:TOK, :]
        left = left + extra[TOK:TOK + 8, :]
        right = right + extra[TOK + 8:, :TOK - D]
    sums[:TOK, :] = start

    def body(t, carry):
        part = pl.ds(pl.multiple_of(t * TILE, TILE), TILE)
        sums[:TOK, :] += lax.dot_general(pick[part, :], rows[part, :], (((0,), (0,)), ((), ())), preferred_element_type=F32)
        return carry

    lax.fori_loop(0, (total + (TILE - 1)) // TILE, body, 0)
    if final:
        dx_out[...] = sums[:TOK, :].astype(BF16)
        dg_out[:, :D] = left
        dg_out[:, D:] = right
    else:
        sums[TOK:TOK + 8, :] = left
        sums[TOK + 8:, :] = jnp.zeros((8, D), F32)
        sums[TOK + 8:, :TOK - D] = right


def combine(first, table, dx_rows, dg_rows, base, steps, partner=None, arrived=(), final=None, mb=0):
    pos, ids, counts = table
    smem = pl.BlockSpec(memory_space=pltpu.SMEM)
    anywhere = pl.BlockSpec(memory_space=pl.ANY)
    block = pl.BlockSpec((None, EXP, TOK), lambda i: (base + 2 * i, 0, 0))
    whole = pl.BlockSpec((SUM_ROWS, D), lambda i: (0, 0))
    extra_specs = [] if partner is None else [pl.BlockSpec((None, SUM_ROWS, D), lambda i: (base // 2, 0, 0))]
    extra_specs += [whole] * len(arrived)
    extra = ([] if partner is None else [partner]) + list(arrived)
    scratch = [
        pltpu.VMEM((ROWS + TILE, TOK), BF16),
        pltpu.VMEM((ROWS + TILE, D), BF16),
        pltpu.VMEM((2, EXP, CAP, D), BF16),
        pltpu.VMEM((2, EXP, CAP, 128), F32),
        pltpu.SemaphoreType.DMA((2,)),
    ]
    in_specs = [smem, smem] + [anywhere] * (2 * N_CHUNK) + [block, block] + extra_specs
    operands = [first, counts, *dx_rows, *dg_rows, pos, ids, *extra]
    mode, aliases = 0, {}
    if final is None:
        if steps > 1:
            outs = jax.ShapeDtypeStruct((steps, SUM_ROWS, D), F32)
            out_specs = pl.BlockSpec((None, SUM_ROWS, D), lambda i: (i, 0, 0))
        else:
            outs, out_specs = jax.ShapeDtypeStruct((SUM_ROWS, D), F32), whole
    else:
        outs = (jax.ShapeDtypeStruct((MICRO, TOK, D), BF16), jax.ShapeDtypeStruct((MICRO, TOP_K, TOK), F32))
        out_specs = (pl.BlockSpec((None, TOK, D), lambda i: (mb, 0, 0)), pl.BlockSpec((None, TOP_K, TOK), lambda i: (mb, 0, 0)))
        scratch = [pltpu.VMEM((TOK, D), F32)] + scratch
        mode = 1
        if final:
            mode = 2
            aliases = {len(operands): 0, len(operands) + 1: 1}
            in_specs += [anywhere, anywhere]
            operands += list(final)
    return pl.pallas_call(
        functools.partial(combine_kernel, base, steps, len(extra), mode),
        grid=(steps,),
        out_shape=outs,
        in_specs=in_specs,
        out_specs=out_specs,
        scratch_shapes=scratch,
        input_output_aliases=aliases,
        compiler_params=params(),
        name="combine",
        cost_estimate=pl.CostEstimate(flops=steps * 2 * ROWS * TOK * D, bytes_accessed=steps * (8 << 20), transcendentals=0),
    )(*operands)


SWAP = [(0, 1), (1, 0)]


def swap(value, axis):
    return lax.ppermute(value, axis, SWAP)


def solution(mesh):
    cube = Mesh(mesh.devices.reshape(2, 2, 2, 2), ('z', 'y', 'x', 'c'))
    tok_spec = P(None, ('z', 'y', 'x', 'c'), None)
    spec_edf = P(('x', 'c'), ('z', 'y'), None)
    spec_efd = P(('x', 'c'), None, ('z', 'y'))

    def gather_tokens(block):
        from_y = swap(block, 'y')
        from_x = swap(block, 'x')
        from_xy = swap(from_y, 'x')
        return [
            block, swap(block, 'c'),
            from_x, swap(from_x, 'c'),
            from_y, swap(from_y, 'c'),
            from_xy, swap(from_xy, 'c'),
        ]

    def local_step(x_in, dy_out, expert_idx, gate_prob, w_one, w_two, w_three):
        z, y, x, c = (lax.axis_index(name) for name in 'zyxc')
        place = jnp.stack([z, y]).astype(jnp.int32)
        first = ((x * 2 + c) * 16 + y * EXP).astype(jnp.int32).reshape(1)
        ids = jnp.swapaxes(expert_idx, 1, 2)
        gate = jnp.swapaxes(gate_prob, 1, 2)

        tokens = [gather_tokens(token_block(x_in, dy_out, ids, gate, mb)) for mb in range(MICRO)]

        w_two_t = jnp.swapaxes(w_two, 1, 2)

        def shard(half, k):
            cut = [lax.dynamic_slice_in_dim(w, half * EXP + STARTS[k], CHUNKS[k], 0) for w in (w_one, w_three, w_two_t)]
            return jnp.concatenate(cut, axis=2)

        pieces = []
        for k in range(N_CHUNK):
            own = shard(y, k)
            from_y = swap(shard(1 - y, k), 'y')
            from_z = swap(own, 'z')
            from_yz = swap(from_y, 'z')
            pieces.append((own, from_y, from_z, from_yz))

        tables = [routing(first, tokens[mb]) for mb in range(MICRO)]
        split = STARTS[2]

        def gather(mb, lo, n):
            pos, gate_sel, _, counts = tables[mb]
            return gather_rows(counts, tokens[mb], pos, gate_sel, lo, n)

        whole = gather(0, 0, EXP)
        head = gather(1, 0, split)
        tail = gather(1, split, EXP - split)

        acc, keep, send = [], [], []
        dx_rows, dg_rows = ([], []), ([], [])
        for k in range(N_CHUNK):
            res = run_experts(place, tables[0][3], whole, STARTS[k], pieces[k], None, k)
            dx_rows[0].append(res[0])
            dg_rows[0].append(res[1])
            acc.append(res[2])
        for k in range(N_CHUNK):
            rows, offset = (head, STARTS[k]) if STARTS[k] < split else (tail, STARTS[k] - split)
            res = run_experts(place, tables[1][3], rows, offset, pieces[k], acc[k], k)
            dx_rows[1].append(res[0])
            dg_rows[1].append(res[1])
            keep.append(res[2])
            send.append(res[3])

        done = ()
        for mb in range(MICRO):
            pos, _, id_table, counts = tables[mb]
            args = (first, (pos, id_table, counts), dx_rows[mb], dg_rows[mb])
            partner = swap(combine(*args, 1, 4), 'c')
            far = swap(combine(*args, 6, 1, partner), 'x')
            near = swap(combine(*args, 2, 1, partner), 'x')
            last = swap(combine(*args, 4, 1, partner, (far,)), 'y')
            done = combine(*args, 0, 1, partner, (near, last), final=done, mb=mb)

        bufs = [jnp.zeros((2 * EXP, QUARTER, F), F32)] * 3
        for k in range(N_CHUNK):
            other = swap(send[k], 'z')

            def cut(which):
                return lax.dynamic_slice_in_dim(keep[k], which * QUARTER, QUARTER, 1) + lax.dynamic_slice_in_dim(other, which * QUARTER, QUARTER, 1)

            theirs = swap(cut(1 - y), 'y')
            mine = cut(y)
            for part in range(3):
                cols = slice(part * F, (part + 1) * F)
                buf = lax.dynamic_update_slice_in_dim(bufs[part], mine[:, :, cols], y * EXP + STARTS[k], 0)
                bufs[part] = lax.dynamic_update_slice_in_dim(buf, theirs[:, :, cols], (1 - y) * EXP + STARTS[k], 0)

        dx_in, d_gate = done
        return dx_in, jnp.swapaxes(d_gate, 1, 2), bufs[0], jnp.swapaxes(bufs[2], 1, 2), bufs[1]

    return jax.shard_map(
        local_step,
        mesh=cube,
        in_specs=(tok_spec, tok_spec, tok_spec, tok_spec, spec_edf, spec_efd, spec_edf),
        out_specs=(tok_spec, tok_spec, spec_edf, spec_efd, spec_edf),
        check_vma=False,
    )
```

profile of v0, /device:TPU:0, one launch (start us, length us, event | category | flops | bytes accessed | tf_op | source)
XLA Modules:
  0.0 1922.4 jit_solution(2732156004358292817)
XLA Ops:
  9.3 80.6 %collective-permute-done.13.refs_4_ = bf16[2112,896]{1,0:T(8,128)(2,1)} collective-permute-done((bf16[2112,896]{1,0:T(8,128)(2,1)}, bf16[2112,896]{1,0:T(8,128)(2,1)}, u32[]{:S(2)}, u32[]{:S(2)}) %collective-permute-start.13) | collective-permute-done | bytes 3784736 | tf_op jit(solution)/shard_map/ppermute | solution.py:528
  92.1 81.0 %collective-permute-done.15.refs_6_ = bf16[2112,896]{1,0:T(8,128)(2,1)} collective-permute-done((bf16[2112,896]{1,0:T(8,128)(2,1)}, bf16[2112,896]{1,0:T(8,128)(2,1)}, u32[]{:S(2)}, u32[]{:S(2)}) %collective-permute-start.15) | collective-permute-done | bytes 3784736 | tf_op jit(solution)/shard_map/ppermute | solution.py:528
  177.2 4.1 constant_dynamic-slice_fusion.4
  191.4 4.1 token_block.2.refs_0_
  212.0 29.8 %collective-permute-done.7.yr_ref = bf16[1,224,1920]{2,1,0:T(8,128)(2,1)} collective-permute-done((bf16[1,224,1920]{2,1,0:T(8,128)(2,1)}, bf16[1,224,1920]{2,1,0:T(8,128)(2,1)}, u32[]{:S(2)}, u32[]{:S(2)}) %collective-permute-start.7) | collective-permute-done | bytes 860192 | tf_op jit(solution)/shard_map/ppermute | solution.py:528
  245.3 52.0 %gather_rows.4 = (bf16[8,1280,896]{2,1,0:T(8,128)(2,1)}, bf16[8,1280,896]{2,1,0:T(8,128)(2,1)}, bf16[8,1280,896]{2,1,0:T(8,128)(2,1)}) custom-call(s32[8,64]{1,0:T(8,128)} %get-tuple-element.67.cnt_ref, bf16[2112,896]{1,0:T(8,128)(2,1)} %token_block.3.refs_0_, bf16[2112,896]{1,0:T(8,128)(2,1)} %collective-permute-done.10.refs_1_, ...), custom_call_target="tpu_custom_call" | custom-call | flops 37580963840 | bytes 90177536 | tf_op jit(solution)/shard_map/gather_rows/pallas_call | solution.py:219
  297.4 80.3 %collective-permute-done.26.yr_ref = bf16[1,224,1920]{2,1,0:T(8,128)(2,1)S(1)} collective-permute-done((bf16[1,224,1920]{2,1,0:T(8,128)(2,1)}, bf16[1,224,1920]{2,1,0:T(8,128)(2,1)S(1)}, u32[]{:S(2)}, u32[]{:S(2)}) %collective-permute-start.26) | collective-permute-done | bytes 860192 | tf_op jit(solution)/shard_map/ppermute | solution.py:528
  383.2 41.3 %experts_first.6 = (bf16[2,1280,896]{2,1,0:T(8,128)(2,1)}, f32[2,1280,128]{2,1,0:T(8,128)}, f32[2,896,1920]{2,1,0:T(8,128)}) custom-call(s32[2]{0:T(128)} %pad_add_fusion.place_ref, s32[8,64]{1,0:T(8,128)} %get-tuple-element.67.cnt_ref, bf16[8,1280,896]{2,1,0:T(8,128)(2,1)} %get-tuple-element.70.x_ref, bf16[8,1280,896]{2,1,0:T(8,128)(2,1)} %get-tuple-element.71.dy_ref, ...), custom_call_target="tpu_custom_call" | custom-call | flops 26424115200 | bytes 50331648 | tf_op jit(solution)/shard_map/experts_first/pallas_call | solution.py:361
  424.5 13.8 collective-permute-done.27.zo_ref
  441.3 33.8 %collective-permute-done.22.zf_ref = bf16[2,224,1920]{2,1,0:T(8,128)(2,1)} collective-permute-done((bf16[2,224,1920]{2,1,0:T(8,128)(2,1)}, bf16[2,224,1920]{2,1,0:T(8,128)(2,1)}, u32[]{:S(2)}, u32[]{:S(2)}) %collective-permute-start.22) | collective-permute-done | bytes 1720352 | tf_op jit(solution)/shard_map/ppermute | solution.py:528
  476.7 34.7 %experts_first.7 = (bf16[2,1280,896]{2,1,0:T(8,128)(2,1)}, f32[2,1280,128]{2,1,0:T(8,128)}, f32[2,896,1920]{2,1,0:T(8,128)}) custom-call(s32[2]{0:T(128)} %pad_add_fusion.place_ref, s32[8,64]{1,0:T(8,128)} %get-tuple-element.67.cnt_ref, bf16[8,1280,896]{2,1,0:T(8,128)(2,1)} %get-tuple-element.70.x_ref, bf16[8,1280,896]{2,1,0:T(8,128)(2,1)} %get-tuple-element.71.dy_ref, ...), custom_call_target="tpu_custom_call" | custom-call | flops 26424115200 | bytes 50331648 | tf_op jit(solution)/shard_map/experts_first/pallas_call | solution.py:361
  511.4 17.4 collective-permute-done.9.zf_ref
  530.8 26.5 %experts_first.5 = (bf16[1,1280,896]{2,1,0:T(8,128)(2,1)}, f32[1,1280,128]{2,1,0:T(8,128)}, f32[1,896,1920]{2,1,0:T(8,128)}) custom-call(s32[2]{0:T(128)} %pad_add_fusion.place_ref, s32[8,64]{1,0:T(8,128)} %get-tuple-element.67.cnt_ref, bf16[8,1280,896]{2,1,0:T(8,128)(2,1)} %get-tuple-element.70.x_ref, bf16[8,1280,896]{2,1,0:T(8,128)(2,1)} %get-tuple-element.71.dy_ref, ...), custom_call_target="tpu_custom_call" | custom-call | flops 13212057600 | bytes 25165824 | tf_op jit(solution)/shard_map/experts_first/pallas_call | solution.py:361
  558.4 19.7 %experts_first.9 = (bf16[1,1280,896]{2,1,0:T(8,128)(2,1)}, f32[1,1280,128]{2,1,0:T(8,128)}, f32[1,896,1920]{2,1,0:T(8,128)}) custom-call(s32[2]{0:T(128)} %pad_add_fusion.place_ref, s32[8,64]{1,0:T(8,128)} %get-tuple-element.67.cnt_ref, bf16[8,1280,896]{2,1,0:T(8,128)(2,1)} %get-tuple-element.70.x_ref, bf16[8,1280,896]{2,1,0:T(8,128)(2,1)} %get-tuple-element.71.dy_ref, ...), custom_call_target="tpu_custom_call" | custom-call | flops 13212057600 | bytes 25165824 | tf_op jit(solution)/shard_map/experts_first/pallas_call | solution.py:361
  578.2 7.1 collective-permute-done.25.zf_ref
  585.3 38.0 %experts_first.8 = (bf16[2,1280,896]{2,1,0:T(8,128)(2,1)}, f32[2,1280,128]{2,1,0:T(8,128)}, f32[2,896,1920]{2,1,0:T(8,128)}) custom-call(s32[2]{0:T(128)} %pad_add_fusion.place_ref, s32[8,64]{1,0:T(8,128)} %get-tuple-element.67.cnt_ref, bf16[8,1280,896]{2,1,0:T(8,128)(2,1)} %get-tuple-element.70.x_ref, bf16[8,1280,896]{2,1,0:T(8,128)(2,1)} %get-tuple-element.71.dy_ref, ...), custom_call_target="tpu_custom_call" | custom-call | flops 26424115200 | bytes 50331648 | tf_op jit(solution)/shard_map/experts_first/pallas_call | solution.py:361
  623.3 22.4 %combine.14 = f32[4,1040,896]{2,1,0:T(8,128)} custom-call(s32[1]{0:T(128)} %bitcast.first_ref, s32[8,64]{1,0:T(8,128)} %get-tuple-element.67.cnt_ref, bf16[1,1280,896]{2,1,0:T(8,128)(2,1)} %get-tuple-element.92.refs_0_, bf16[2,1280,896]{2,1,0:T(8,128)(2,1)} %get-tuple-element.93.refs_1_, bf16[2,1280,896]{2,1,0:T(8,128)(2,1)} %get-tuple-element.94.refs_2_, ...), custom_call_target="tpu_custom_call" | custom-call | flops 9395240960 | bytes 33554432 | tf_op jit(solution)/shard_map/combine/pallas_call | solution.py:510
  649.4 23.6 %gather_rows.3 = (bf16[3,1280,896]{2,1,0:T(8,128)(2,1)}, bf16[3,1280,896]{2,1,0:T(8,128)(2,1)}, bf16[3,1280,896]{2,1,0:T(8,128)(2,1)}) custom-call(s32[8,64]{1,0:T(8,128)} %get-tuple-element.61.cnt_ref, bf16[2112,896]{1,0:T(8,128)(2,1)} %token_block.2.refs_0_, bf16[2112,896]{1,0:T(8,128)(2,1)} %collective-permute-done.refs_1_, ...), custom_call_target="tpu_custom_call" | custom-call | flops 14092861440 | bytes 53477376 | tf_op jit(solution)/shard_map/gather_rows/pallas_call | solution.py:219
  673.0 30.9 %gather_rows.5 = (bf16[5,1280,896]{2,1,0:T(8,128)(2,1)}, bf16[5,1280,896]{2,1,0:T(8,128)(2,1)}, bf16[5,1280,896]{2,1,0:T(8,128)(2,1)}) custom-call(s32[8,64]{1,0:T(8,128)} %get-tuple-element.61.cnt_ref, bf16[2112,896]{1,0:T(8,128)(2,1)} %token_block.2.refs_0_, bf16[2112,896]{1,0:T(8,128)(2,1)} %collective-permute-done.refs_1_, ...), custom_call_target="tpu_custom_call" | custom-call | flops 23488102400 | bytes 68157440 | tf_op jit(solution)/shard_map/gather_rows/pallas_call | solution.py:219
  704.0 21.7 %experts_second.5 = (bf16[1,1280,896]{2,1,0:T(8,128)(2,1)}, f32[1,1280,128]{2,1,0:T(8,128)}, f32[1,448,1920]{2,1,0:T(8,128)}, f32[1,448,1920]{2,1,0:T(8,128)}) custom-call(s32[2]{0:T(128)} %pad_add_fusion.place_ref, s32[8,64]{1,0:T(8,128)} %get-tuple-element.61.cnt_ref, bf16[3,1280,896]{2,1,0:T(8,128)(2,1)} %get-tuple-element.64.x_ref, ...), custom_call_target="tpu_custom_call" | custom-call | flops 13212057600 | bytes 25165824 | tf_op jit(solution)/shard_map/experts_second/pallas_call | solution.py:361
  725.7 40.2 %experts_second.6 = (bf16[2,1280,896]{2,1,0:T(8,128)(2,1)}, f32[2,1280,128]{2,1,0:T(8,128)}, f32[2,448,1920]{2,1,0:T(8,128)}, f32[2,448,1920]{2,1,0:T(8,128)}) custom-call(s32[2]{0:T(128)} %pad_add_fusion.place_ref, s32[8,64]{1,0:T(8,128)} %get-tuple-element.61.cnt_ref, bf16[3,1280,896]{2,1,0:T(8,128)(2,1)} %get-tuple-element.64.x_ref, ...), custom_call_target="tpu_custom_call" | custom-call | flops 26424115200 | bytes 50331648 | tf_op jit(solution)/shard_map/experts_second/pallas_call | solution.py:361
  765.9 40.6 %experts_second.7 = (bf16[2,1280,896]{2,1,0:T(8,128)(2,1)}, f32[2,1280,128]{2,1,0:T(8,128)}, f32[2,448,1920]{2,1,0:T(8,128)}, f32[2,448,1920]{2,1,0:T(8,128)}) custom-call(s32[2]{0:T(128)} %pad_add_fusion.place_ref, s32[8,64]{1,0:T(8,128)} %get-tuple-element.61.cnt_ref, bf16[5,1280,896]{2,1,0:T(8,128)(2,1)} %get-tuple-element.77.x_ref, ...), custom_call_target="tpu_custom_call" | custom-call | flops 26424115200 | bytes 50331648 | tf_op jit(solution)/shard_map/experts_second/pallas_call | solution.py:361
  806.6 40.5 %experts_second.8 = (bf16[2,1280,896]{2,1,0:T(8,128)(2,1)}, f32[2,1280,128]{2,1,0:T(8,128)}, f32[2,448,1920]{2,1,0:T(8,128)}, f32[2,448,1920]{2,1,0:T(8,128)}) custom-call(s32[2]{0:T(128)} %pad_add_fusion.place_ref, s32[8,64]{1,0:T(8,128)} %get-tuple-element.61.cnt_ref, bf16[5,1280,896]{2,1,0:T(8,128)(2,1)} %get-tuple-element.77.x_ref, ...), custom_call_target="tpu_custom_call" | custom-call | flops 26424115200 | bytes 50331648 | tf_op jit(solution)/shard_map/experts_second/pallas_call | solution.py:361
  847.1 21.6 %experts_second.9 = (bf16[1,1280,896]{2,1,0:T(8,128)(2,1)}, f32[1,1280,128]{2,1,0:T(8,128)}, f32[1,448,1920]{2,1,0:T(8,128)}, f32[1,448,1920]{2,1,0:T(8,128)}) custom-call(s32[2]{0:T(128)} %pad_add_fusion.place_ref, s32[8,64]{1,0:T(8,128)} %get-tuple-element.61.cnt_ref, bf16[5,1280,896]{2,1,0:T(8,128)(2,1)} %get-tuple-element.77.x_ref, ...), custom_call_target="tpu_custom_call" | custom-call | flops 13212057600 | bytes 25165824 | tf_op jit(solution)/shard_map/experts_second/pallas_call | solution.py:361
  868.7 22.0 %combine.10 = f32[4,1040,896]{2,1,0:T(8,128)} custom-call(s32[1]{0:T(128)} %bitcast.first_ref, s32[8,64]{1,0:T(8,128)} %get-tuple-element.61.cnt_ref, bf16[1,1280,896]{2,1,0:T(8,128)(2,1)} %get-tuple-element.74.refs_0_, bf16[2,1280,896]{2,1,0:T(8,128)(2,1)} %get-tuple-element.76.refs_1_, bf16[2,1280,896]{2,1,0:T(8,128)(2,1)} %get-tuple-element.81.refs_2_, ...), custom_call_target="tpu_custom_call" | custom-call | flops 9395240960 | bytes 33554432 | tf_op jit(solution)/shard_map/combine/pallas_call | solution.py:510
  890.7 23.5 %collective-permute-start.29 = (f32[4,1040,896]{2,1,0:T(8,128)}, f32[4,1040,896]{2,1,0:T(8,128)}, u32[]{:S(2)}, u32[]{:S(2)}) collective-permute-start(f32[4,1040,896]{2,1,0:T(8,128)} %combine.10), channel_id=1, source_target_pairs={{0,1},{1,0},{2,3},{3,2},{4,5},{5,4},{6,7},{7,6},{8,9},{9,8},{10,11... | collective-permute-start | bytes 44728328 | tf_op jit(solution)/shard_map/ppermute | solution.py:528
  916.3 149.3 %collective-permute-done.39 = f32[2,448,1920]{2,1,0:T(8,128)} collective-permute-done((f32[2,448,1920]{2,1,0:T(8,128)}, f32[2,448,1920]{2,1,0:T(8,128)}, u32[]{:S(2)}, u32[]{:S(2)}) %collective-permute-start.39) | collective-permute-done | bytes 6881312 | tf_op jit(solution)/shard_map/ppermute | solution.py:528
  1067.6 10.2 combine.16
  1077.9 9.8 combine.12
  1087.6 125.4 %collective-permute-done.41 = f32[2,448,1920]{2,1,0:T(8,128)} collective-permute-done((f32[2,448,1920]{2,1,0:T(8,128)}, f32[2,448,1920]{2,1,0:T(8,128)}, u32[]{:S(2)}, u32[]{:S(2)}) %collective-permute-start.41) | collective-permute-done | bytes 6881312 | tf_op jit(solution)/shard_map/ppermute | solution.py:528
  1213.0 8.5 dynamic-slice_add_fusion.4
  1221.6 8.7 dynamic-slice_add_fusion.2
  1230.2 204.0 %collective-permute-done.37 = f32[1,448,1920]{2,1,0:T(8,128)} collective-permute-done((f32[1,448,1920]{2,1,0:T(8,128)}, f32[1,448,1920]{2,1,0:T(8,128)}, u32[]{:S(2)}, u32[]{:S(2)}) %collective-permute-start.37) | collective-permute-done | bytes 3440672 | tf_op jit(solution)/shard_map/ppermute | solution.py:528
  1436.3 6.7 dynamic-slice_add_fusion
  1442.9 64.1 %collective-permute-done.45 = f32[1,448,1920]{2,1,0:T(8,128)} collective-permute-done((f32[1,448,1920]{2,1,0:T(8,128)}, f32[1,448,1920]{2,1,0:T(8,128)}, u32[]{:S(2)}, u32[]{:S(2)}) %collective-permute-start.45) | collective-permute-done | bytes 3440672 | tf_op jit(solution)/shard_map/ppermute | solution.py:528
  1512.6 4.6 broadcast_in_dim.3.clone
  1518.1 10.9 combine.15
  1528.9 9.4 combine.11
  1538.4 11.4 combine.17
  1549.7 143.7 %collective-permute-done.38 = f32[1,224,1920]{2,1,0:T(8,128)} collective-permute-done((f32[1,224,1920]{2,1,0:T(8,128)}, f32[1,224,1920]{2,1,0:T(8,128)}, u32[]{:S(2)}, u32[]{:S(2)}) %collective-permute-start.38) | collective-permute-done | bytes 1720352 | tf_op jit(solution)/shard_map/ppermute | solution.py:528
  1693.5 8.2 collective-permute-start.34
  1703.4 10.7 combine.13
  1715.3 4.6 broadcast_in_dim.3.clone.1
  1720.7 4.6 broadcast_in_dim.3.clone.2
  1734.9 3.9 slice_dynamic-update-slice_fusion.4
  1751.5 147.0 %collective-permute-done.46 = f32[1,224,1920]{2,1,0:T(8,128)S(1)} collective-permute-done((f32[1,224,1920]{2,1,0:T(8,128)S(1)}, f32[1,224,1920]{2,1,0:T(8,128)S(1)}, u32[]{:S(2)}, u32[]{:S(2)}) %collective-permute-start.46) | collective-permute-done | bytes 1720352 | tf_op jit(solution)/shard_map/ppermute | solution.py:528
  1899.7 11.6 combine.18
  1911.3 10.8 combine.19
  (161 shorter events, 101.7 us)
Async XLA Ops:
  4.5 85.4 %collective-permute-start.13 = (bf16[2112,896]{1,0:T(8,128)(2,1)}, bf16[2112,896]{1,0:T(8,128)(2,1)}, u32[]{:S(2)}, u32[]{:S(2)}) collective-permute-start(bf16[2112,896]{1,0:T(8,128)(2,1)} %token_block.3.refs_0_), channel_id=1, source_target_pairs={{0,4},{4,0},{1,5},{5,1},{2,6},{6,2},{3,7},{7,3},{8,12},{12,8},{9,1... | collective-permute-start | bytes 11354120 | tf_op jit(solution)/shard_map/ppermute | solution.py:528
  7.8 84.3 %collective-permute-start.11 = (bf16[2112,896]{1,0:T(8,128)(2,1)}, bf16[2112,896]{1,0:T(8,128)(2,1)}, u32[]{:S(2)}, u32[]{:S(2)}) collective-permute-start(bf16[2112,896]{1,0:T(8,128)(2,1)} %token_block.3.refs_0_), channel_id=1, source_target_pairs={{0,2},{2,0},{1,3},{3,1},{4,6},{6,4},{5,7},{7,5},{8,10},{10,8},{9,1... | collective-permute-start | bytes 11354120 | tf_op jit(solution)/shard_map/ppermute | solution.py:528
  89.9 83.3 %collective-permute-start.15 = (bf16[2112,896]{1,0:T(8,128)(2,1)}, bf16[2112,896]{1,0:T(8,128)(2,1)}, u32[]{:S(2)}, u32[]{:S(2)}) collective-permute-start(bf16[2112,896]{1,0:T(8,128)(2,1)} %collective-permute-done.13.refs_4_), channel_id=1, source_target_pairs={{0,2},{2,0},{1,3},{3,1},{4,6},{6,4},{5,7},{7,5},{8,10},{10,8},{9,1... | collective-permute-start | bytes 11354120 | tf_op jit(solution)/shard_map/ppermute | solution.py:528
  91.6 109.5 %collective-permute-start.10 = (bf16[2112,896]{1,0:T(8,128)(2,1)}, bf16[2112,896]{1,0:T(8,128)(2,1)}, u32[]{:S(2)}, u32[]{:S(2)}) collective-permute-start(bf16[2112,896]{1,0:T(8,128)(2,1)} %token_block.3.refs_0_), channel_id=1, source_target_pairs={{0,1},{1,0},{2,3},{3,2},{4,5},{5,4},{6,7},{7,6},{8,9},{9,8},{10,11... | collective-permute-start | bytes 11354120 | tf_op jit(solution)/shard_map/ppermute | solution.py:528
  91.6 110.1 %collective-permute-start.14 = (bf16[2112,896]{1,0:T(8,128)(2,1)}, bf16[2112,896]{1,0:T(8,128)(2,1)}, u32[]{:S(2)}, u32[]{:S(2)}) collective-permute-start(bf16[2112,896]{1,0:T(8,128)(2,1)} %collective-permute-done.13.refs_4_), channel_id=1, source_target_pairs={{0,1},{1,0},{2,3},{3,2},{4,5},{5,4},{6,7},{7,6},{8,9},{9,8},{10,11... | collective-permute-start | bytes 11354120 | tf_op jit(solution)/shard_map/ppermute | solution.py:528
  92.1 113.5 %collective-permute-start.12 = (bf16[2112,896]{1,0:T(8,128)(2,1)}, bf16[2112,896]{1,0:T(8,128)(2,1)}, u32[]{:S(2)}, u32[]{:S(2)}) collective-permute-start(bf16[2112,896]{1,0:T(8,128)(2,1)} %collective-permute-done.11.refs_2_), channel_id=1, source_target_pairs={{0,1},{1,0},{2,3},{3,2},{4,5},{5,4},{6,7},{7,6},{8,9},{9,8},{10,11... | collective-permute-start | bytes 11354120 | tf_op jit(solution)/shard_map/ppermute | solution.py:528
  173.2 34.7 %collective-permute-start.16 = (bf16[2112,896]{1,0:T(8,128)(2,1)}, bf16[2112,896]{1,0:T(8,128)(2,1)}, u32[]{:S(2)}, u32[]{:S(2)}) collective-permute-start(bf16[2112,896]{1,0:T(8,128)(2,1)} %collective-permute-done.15.refs_6_), channel_id=1, source_target_pairs={{0,1},{1,0},{2,3},{3,2},{4,5},{5,4},{6,7},{7,6},{8,9},{9,8},{10,11... | collective-permute-start | bytes 11354120 | tf_op jit(solution)/shard_map/ppermute | solution.py:528
  182.6 61.2 %collective-permute-start.17 = (bf16[2,224,1920]{2,1,0:T(8,128)(2,1)}, bf16[2,224,1920]{2,1,0:T(8,128)(2,1)}, u32[]{:S(2)}, u32[]{:S(2)}) collective-permute-start(bf16[2,224,1920]{2,1,0:T(8,128)(2,1)} %pad_maximum_fusion.1), channel_id=1, source_target_pairs={{0,4},{4,0},{1,5},{5,1},{2,6},{6,2},{3,7},{7,3},{8,12},{12,8},{9,1... | collective-permute-start | bytes 5160968 | tf_op jit(solution)/shard_map/ppermute | solution.py:528
  201.1 40.7 %collective-permute-start.7 = (bf16[1,224,1920]{2,1,0:T(8,128)(2,1)}, bf16[1,224,1920]{2,1,0:T(8,128)(2,1)}, u32[]{:S(2)}, u32[]{:S(2)}) collective-permute-start(bf16[1,224,1920]{2,1,0:T(8,128)(2,1)} %pad_maximum_fusion.7), channel_id=1, source_target_pairs={{0,4},{4,0},{1,5},{5,1},{2,6},{6,2},{3,7},{7,3},{8,12},{12,8},{9,1... | collective-permute-start | bytes 2580488 | tf_op jit(solution)/shard_map/ppermute | solution.py:528
  201.7 41.5 %collective-permute-start.8 = (bf16[1,224,1920]{2,1,0:T(8,128)(2,1)S(1)}, bf16[1,224,1920]{2,1,0:T(8,128)(2,1)}, u32[]{:S(2)}, u32[]{:S(2)}) collective-permute-start(bf16[1,224,1920]{2,1,0:T(8,128)(2,1)S(1)} %pad_maximum_fusion.6.own_ref), channel_id=1, source_target_pairs={{0,8},{8,0},{1,9},{9,1},{2,10},{10,2},{3,11},{11,3},{4,12},{12,4},... | collective-permute-start | bytes 2580488 | tf_op jit(solution)/shard_map/ppermute | solution.py:528
  205.7 177.0 %collective-permute-start.3 = (bf16[2112,896]{1,0:T(8,128)(2,1)}, bf16[2112,896]{1,0:T(8,128)(2,1)}, u32[]{:S(2)}, u32[]{:S(2)}) collective-permute-start(bf16[2112,896]{1,0:T(8,128)(2,1)} %token_block.2.refs_0_), channel_id=1, source_target_pairs={{0,4},{4,0},{1,5},{5,1},{2,6},{6,2},{3,7},{7,3},{8,12},{12,8},{9,1... | collective-permute-start | bytes 11354120 | tf_op jit(solution)/shard_map/ppermute | solution.py:528
  207.9 171.2 %collective-permute-start.18 = (bf16[2,224,1920]{2,1,0:T(8,128)(2,1)}, bf16[2,224,1920]{2,1,0:T(8,128)(2,1)}, u32[]{:S(2)}, u32[]{:S(2)}) collective-permute-start(bf16[2,224,1920]{2,1,0:T(8,128)(2,1)} %pad_maximum_fusion.own_ref), channel_id=1, source_target_pairs={{0,8},{8,0},{1,9},{9,1},{2,10},{10,2},{3,11},{11,3},{4,12},{12,4},... | collective-permute-start | bytes 5160968 | tf_op jit(solution)/shard_map/ppermute | solution.py:528
  241.8 138.9 %collective-permute-start.20 = (bf16[2,224,1920]{2,1,0:T(8,128)(2,1)}, bf16[2,224,1920]{2,1,0:T(8,128)(2,1)}, u32[]{:S(2)}, u32[]{:S(2)}) collective-permute-start(bf16[2,224,1920]{2,1,0:T(8,128)(2,1)} %pad_maximum_fusion.3), channel_id=1, source_target_pairs={{0,4},{4,0},{1,5},{5,1},{2,6},{6,2},{3,7},{7,3},{8,12},{12,8},{9,1... | collective-permute-start | bytes 5160968 | tf_op jit(solution)/shard_map/ppermute | solution.py:528
  243.2 134.4 %collective-permute-start.26 = (bf16[1,224,1920]{2,1,0:T(8,128)(2,1)}, bf16[1,224,1920]{2,1,0:T(8,128)(2,1)S(1)}, u32[]{:S(2)}, u32[]{:S(2)}) collective-permute-start(bf16[1,224,1920]{2,1,0:T(8,128)(2,1)} %pad_maximum_fusion.9), channel_id=1, source_target_pairs={{0,4},{4,0},{1,5},{5,1},{2,6},{6,2},{3,7},{7,3},{8,12},{12,8},{9,1... | collective-permute-start | bytes 2580488 | tf_op jit(solution)/shard_map/ppermute | solution.py:528
  243.8 137.3 %collective-permute-start.19 = (bf16[2,224,1920]{2,1,0:T(8,128)(2,1)}, bf16[2,224,1920]{2,1,0:T(8,128)(2,1)}, u32[]{:S(2)}, u32[]{:S(2)}) collective-permute-start(bf16[2,224,1920]{2,1,0:T(8,128)(2,1)} %collective-permute-done.17.yr_ref), channel_id=1, source_target_pairs={{0,8},{8,0},{1,9},{9,1},{2,10},{10,2},{3,11},{11,3},{4,12},{12,4},... | collective-permute-start | bytes 5160968 | tf_op jit(solution)/shard_map/ppermute | solution.py:528
  377.6 180.3 %collective-permute-start.1 = (bf16[2112,896]{1,0:T(8,128)(2,1)}, bf16[2112,896]{1,0:T(8,128)(2,1)}, u32[]{:S(2)}, u32[]{:S(2)}) collective-permute-start(bf16[2112,896]{1,0:T(8,128)(2,1)} %token_block.2.refs_0_), channel_id=1, source_target_pairs={{0,2},{2,0},{1,3},{3,1},{4,6},{6,4},{5,7},{7,5},{8,10},{10,8},{9,1... | collective-permute-start | bytes 11354120 | tf_op jit(solution)/shard_map/ppermute | solution.py:528
  379.1 60.7 %collective-permute-start.21 = (bf16[2,224,1920]{2,1,0:T(8,128)(2,1)}, bf16[2,224,1920]{2,1,0:T(8,128)(2,1)}, u32[]{:S(2)}, u32[]{:S(2)}) collective-permute-start(bf16[2,224,1920]{2,1,0:T(8,128)(2,1)} %pad_maximum_fusion.2.own_ref), channel_id=1, source_target_pairs={{0,8},{8,0},{1,9},{9,1},{2,10},{10,2},{3,11},{11,3},{4,12},{12,4},... | collective-permute-start | bytes 5160968 | tf_op jit(solution)/shard_map/ppermute | solution.py:528
  380.6 57.6 %collective-permute-start.27 = (bf16[1,224,1920]{2,1,0:T(8,128)(2,1)S(1)}, bf16[1,224,1920]{2,1,0:T(8,128)(2,1)}, u32[]{:S(2)}, u32[]{:S(2)}) collective-permute-start(bf16[1,224,1920]{2,1,0:T(8,128)(2,1)S(1)} %pad_maximum_fusion.8.own_ref), channel_id=1, source_target_pairs={{0,8},{8,0},{1,9},{9,1},{2,10},{10,2},{3,11},{11,3},{4,12},{12,4},... | collective-permute-start | bytes 2580488 | tf_op jit(solution)/shard_map/ppermute | solution.py:528
  381.1 94.0 %collective-permute-start.22 = (bf16[2,224,1920]{2,1,0:T(8,128)(2,1)}, bf16[2,224,1920]{2,1,0:T(8,128)(2,1)}, u32[]{:S(2)}, u32[]{:S(2)}) collective-permute-start(bf16[2,224,1920]{2,1,0:T(8,128)(2,1)} %collective-permute-done.20.yr_ref), channel_id=1, source_target_pairs={{0,8},{8,0},{1,9},{9,1},{2,10},{10,2},{3,11},{11,3},{4,12},{12,4},... | collective-permute-start | bytes 5160968 | tf_op jit(solution)/shard_map/ppermute | solution.py:528
  382.7 175.3 %collective-permute-start.5 = (bf16[2112,896]{1,0:T(8,128)(2,1)}, bf16[2112,896]{1,0:T(8,128)(2,1)}, u32[]{:S(2)}, u32[]{:S(2)}) collective-permute-start(bf16[2112,896]{1,0:T(8,128)(2,1)} %collective-permute-done.3.refs_4_), channel_id=1, source_target_pairs={{0,2},{2,0},{1,3},{3,1},{4,6},{6,4},{5,7},{7,5},{8,10},{10,8},{9,1... | collective-permute-start | bytes 11354120 | tf_op jit(solution)/shard_map/ppermute | solution.py:528
  438.2 92.2 %collective-permute-start.23 = (bf16[2,224,1920]{2,1,0:T(8,128)(2,1)}, bf16[2,224,1920]{2,1,0:T(8,128)(2,1)}, u32[]{:S(2)}, u32[]{:S(2)}) collective-permute-start(bf16[2,224,1920]{2,1,0:T(8,128)(2,1)} %pad_maximum_fusion.5), channel_id=1, source_target_pairs={{0,4},{4,0},{1,5},{5,1},{2,6},{6,2},{3,7},{7,3},{8,12},{12,8},{9,1... | collective-permute-start | bytes 5160968 | tf_op jit(solution)/shard_map/ppermute | solution.py:528
  439.8 117.6 %collective-permute-start.24 = (bf16[2,224,1920]{2,1,0:T(8,128)(2,1)}, bf16[2,224,1920]{2,1,0:T(8,128)(2,1)}, u32[]{:S(2)}, u32[]{:S(2)}) collective-permute-start(bf16[2,224,1920]{2,1,0:T(8,128)(2,1)} %pad_maximum_fusion.4.own_ref), channel_id=1, source_target_pairs={{0,8},{8,0},{1,9},{9,1},{2,10},{10,2},{3,11},{11,3},{4,12},{12,4},... | collective-permute-start | bytes 5160968 | tf_op jit(solution)/shard_map/ppermute | solution.py:528
  475.1 53.7 %collective-permute-start.9 = (bf16[1,224,1920]{2,1,0:T(8,128)(2,1)}, bf16[1,224,1920]{2,1,0:T(8,128)(2,1)}, u32[]{:S(2)}, u32[]{:S(2)}) collective-permute-start(bf16[1,224,1920]{2,1,0:T(8,128)(2,1)} %collective-permute-done.7.yr_ref), channel_id=1, source_target_pairs={{0,8},{8,0},{1,9},{9,1},{2,10},{10,2},{3,11},{11,3},{4,12},{12,4},... | collective-permute-start | bytes 2580488 | tf_op jit(solution)/shard_map/ppermute | solution.py:528
  528.8 28.6 %collective-permute-start.28 = (bf16[1,224,1920]{2,1,0:T(8,128)(2,1)S(1)}, bf16[1,224,1920]{2,1,0:T(8,128)(2,1)S(1)}, u32[]{:S(2)}, u32[]{:S(2)}) collective-permute-start(bf16[1,224,1920]{2,1,0:T(8,128)(2,1)S(1)} %collective-permute-done.26.yr_ref), channel_id=1, source_target_pairs={{0,8},{8,0},{1,9},{9,1},{2,10},{10,2},{3,11},{11,3},{4,12},{12,4},... | collective-permute-start | bytes 2580488 | tf_op jit(solution)/shard_map/ppermute | solution.py:528
  530.4 54.9 %collective-permute-start.25 = (bf16[2,224,1920]{2,1,0:T(8,128)(2,1)}, bf16[2,224,1920]{2,1,0:T(8,128)(2,1)}, u32[]{:S(2)}, u32[]{:S(2)}) collective-permute-start(bf16[2,224,1920]{2,1,0:T(8,128)(2,1)} %collective-permute-done.23.yr_ref), channel_id=1, source_target_pairs={{0,8},{8,0},{1,9},{9,1},{2,10},{10,2},{3,11},{11,3},{4,12},{12,4},... | collective-permute-start | bytes 5160968 | tf_op jit(solution)/shard_map/ppermute | solution.py:528
  557.4 88.4 %collective-permute-start = (bf16[2112,896]{1,0:T(8,128)(2,1)}, bf16[2112,896]{1,0:T(8,128)(2,1)}, u32[]{:S(2)}, u32[]{:S(2)}) collective-permute-start(bf16[2112,896]{1,0:T(8,128)(2,1)} %token_block.2.refs_0_), channel_id=1, source_target_pairs={{0,1},{1,0},{2,3},{3,2},{4,5},{5,4},{6,7},{7,6},{8,9},{9,8},{10,11... | collective-permute-start | bytes 11354120 | tf_op jit(solution)/shard_map/ppermute | solution.py:528
  557.4 88.3 %collective-permute-start.4 = (bf16[2112,896]{1,0:T(8,128)(2,1)}, bf16[2112,896]{1,0:T(8,128)(2,1)}, u32[]{:S(2)}, u32[]{:S(2)}) collective-permute-start(bf16[2112,896]{1,0:T(8,128)(2,1)} %collective-permute-done.3.refs_4_), channel_id=1, source_target_pairs={{0,1},{1,0},{2,3},{3,2},{4,5},{5,4},{6,7},{7,6},{8,9},{9,8},{10,11... | collective-permute-start | bytes 11354120 | tf_op jit(solution)/shard_map/ppermute | solution.py:528
  557.9 87.8 %collective-permute-start.2 = (bf16[2112,896]{1,0:T(8,128)(2,1)}, bf16[2112,896]{1,0:T(8,128)(2,1)}, u32[]{:S(2)}, u32[]{:S(2)}) collective-permute-start(bf16[2112,896]{1,0:T(8,128)(2,1)} %collective-permute-done.1.refs_2_), channel_id=1, source_target_pairs={{0,1},{1,0},{2,3},{3,2},{4,5},{5,4},{6,7},{7,6},{8,9},{9,8},{10,11... | collective-permute-start | bytes 11354120 | tf_op jit(solution)/shard_map/ppermute | solution.py:528
  558.0 87.8 %collective-permute-start.6 = (bf16[2112,896]{1,0:T(8,128)(2,1)}, bf16[2112,896]{1,0:T(8,128)(2,1)}, u32[]{:S(2)}, u32[]{:S(2)}) collective-permute-start(bf16[2112,896]{1,0:T(8,128)(2,1)} %collective-permute-done.5.refs_6_), channel_id=1, source_target_pairs={{0,1},{1,0},{2,3},{3,2},{4,5},{5,4},{6,7},{7,6},{8,9},{9,8},{10,11... | collective-permute-start | bytes 11354120 | tf_op jit(solution)/shard_map/ppermute | solution.py:528
  645.7 419.9 %collective-permute-start.33 = (f32[4,1040,896]{2,1,0:T(8,128)}, f32[4,1040,896]{2,1,0:T(8,128)}, u32[]{:S(2)}, u32[]{:S(2)}) collective-permute-start(f32[4,1040,896]{2,1,0:T(8,128)} %combine.14), channel_id=1, source_target_pairs={{0,1},{1,0},{2,3},{3,2},{4,5},{5,4},{6,7},{7,6},{8,9},{9,8},{10,11... | collective-permute-start | bytes 44728328 | tf_op jit(solution)/shard_map/ppermute | solution.py:528
  890.7 187.1 %collective-permute-start.29 = (f32[4,1040,896]{2,1,0:T(8,128)}, f32[4,1040,896]{2,1,0:T(8,128)}, u32[]{:S(2)}, u32[]{:S(2)}) collective-permute-start(f32[4,1040,896]{2,1,0:T(8,128)} %combine.10), channel_id=1, source_target_pairs={{0,1},{1,0},{2,3},{3,2},{4,5},{5,4},{6,7},{7,6},{8,9},{9,8},{10,11... | collective-permute-start | bytes 44728328 | tf_op jit(solution)/shard_map/ppermute | solution.py:528
  914.2 151.3 %collective-permute-start.39 = (f32[2,448,1920]{2,1,0:T(8,128)}, f32[2,448,1920]{2,1,0:T(8,128)}, u32[]{:S(2)}, u32[]{:S(2)}) collective-permute-start(f32[2,448,1920]{2,1,0:T(8,128)} %get-tuple-element.110), channel_id=1, source_target_pairs={{0,8},{8,0},{1,9},{9,1},{2,10},{10,2},{3,11},{11,3},{4,12},{12,4},... | collective-permute-start | bytes 20643848 | tf_op jit(solution)/shard_map/ppermute | solution.py:528
  914.2 298.8 %collective-permute-start.41 = (f32[2,448,1920]{2,1,0:T(8,128)}, f32[2,448,1920]{2,1,0:T(8,128)}, u32[]{:S(2)}, u32[]{:S(2)}) collective-permute-start(f32[2,448,1920]{2,1,0:T(8,128)} %get-tuple-element.112), channel_id=1, source_target_pairs={{0,8},{8,0},{1,9},{9,1},{2,10},{10,2},{3,11},{11,3},{4,12},{12,4},... | collective-permute-start | bytes 20643848 | tf_op jit(solution)/shard_map/ppermute | solution.py:528
  916.3 518.0 %collective-permute-start.43 = (f32[2,448,1920]{2,1,0:T(8,128)}, f32[2,448,1920]{2,1,0:T(8,128)}, u32[]{:S(2)}, u32[]{:S(2)}) collective-permute-start(f32[2,448,1920]{2,1,0:T(8,128)} %get-tuple-element.114), channel_id=1, source_target_pairs={{0,8},{8,0},{1,9},{9,1},{2,10},{10,2},{3,11},{11,3},{4,12},{12,4},... | collective-permute-start | bytes 20643848 | tf_op jit(solution)/shard_map/ppermute | solution.py:528
  1065.6 368.7 %collective-permute-start.37 = (f32[1,448,1920]{2,1,0:T(8,128)}, f32[1,448,1920]{2,1,0:T(8,128)}, u32[]{:S(2)}, u32[]{:S(2)}) collective-permute-start(f32[1,448,1920]{2,1,0:T(8,128)} %get-tuple-element.108), channel_id=1, source_target_pairs={{0,8},{8,0},{1,9},{9,1},{2,10},{10,2},{3,11},{11,3},{4,12},{12,4},... | collective-permute-start | bytes 10321928 | tf_op jit(solution)/shard_map/ppermute | solution.py:528
  1065.6 441.5 %collective-permute-start.45 = (f32[1,448,1920]{2,1,0:T(8,128)}, f32[1,448,1920]{2,1,0:T(8,128)}, u32[]{:S(2)}, u32[]{:S(2)}) collective-permute-start(f32[1,448,1920]{2,1,0:T(8,128)} %get-tuple-element.116), channel_id=1, source_target_pairs={{0,8},{8,0},{1,9},{9,1},{2,10},{10,2},{3,11},{11,3},{4,12},{12,4},... | collective-permute-start | bytes 10321928 | tf_op jit(solution)/shard_map/ppermute | solution.py:528
  1077.8 432.8 %collective-permute-start.35 = (f32[1040,896]{1,0:T(8,128)}, f32[1040,896]{1,0:T(8,128)}, u32[]{:S(2)}, u32[]{:S(2)}) collective-permute-start(f32[1040,896]{1,0:T(8,128)} %combine.16), channel_id=1, source_target_pairs={{0,2},{2,0},{1,3},{3,1},{4,6},{6,4},{5,7},{7,5},{8,10},{10,8},{9,1... | collective-permute-start | bytes 11182088 | tf_op jit(solution)/shard_map/ppermute | solution.py:528
  1213.0 488.6 %collective-permute-start.31 = (f32[1040,896]{1,0:T(8,128)}, f32[1040,896]{1,0:T(8,128)}, u32[]{:S(2)}, u32[]{:S(2)}) collective-permute-start(f32[1040,896]{1,0:T(8,128)} %combine.12), channel_id=1, source_target_pairs={{0,2},{2,0},{1,3},{3,1},{4,6},{6,4},{5,7},{7,5},{8,10},{10,8},{9,1... | collective-permute-start | bytes 11182088 | tf_op jit(solution)/shard_map/ppermute | solution.py:528
  1221.6 214.7 %slice-start.1 = ((s8[6881280]{0:T(1024)(128)(4,1)}), s8[2686976]{0:T(1024)(128)(4,1)S(1)}, s32[]{:S(2)}) async-start(s8[6881280]{0:T(1024)(128)(4,1)} %bitcast.27), calls=%async_computation.1 | async-start | bytes 5373952
  1434.2 279.9 %collective-permute-start.40 = (f32[2,224,1920]{2,1,0:T(8,128)}, f32[2,224,1920]{2,1,0:T(8,128)}, u32[]{:S(2)}, u32[]{:S(2)}) collective-permute-start(f32[2,224,1920]{2,1,0:T(8,128)} %get-tuple-element.121), channel_id=1, source_target_pairs={{0,4},{4,0},{1,5},{5,1},{2,6},{6,2},{3,7},{7,3},{8,12},{12,8},{9,1... | collective-permute-start | bytes 10321928 | tf_op jit(solution)/shard_map/ppermute | solution.py:528
  1434.2 280.7 %collective-permute-start.42 = (f32[2,224,1920]{2,1,0:T(8,128)}, f32[2,224,1920]{2,1,0:T(8,128)}, u32[]{:S(2)}, u32[]{:S(2)}) collective-permute-start(f32[2,224,1920]{2,1,0:T(8,128)} %get-tuple-element.119), channel_id=1, source_target_pairs={{0,4},{4,0},{1,5},{5,1},{2,6},{6,2},{3,7},{7,3},{8,12},{12,8},{9,1... | collective-permute-start | bytes 10321928 | tf_op jit(solution)/shard_map/ppermute | solution.py:528
  1507.1 226.2 %collective-permute-start.44 = (f32[2,224,1920]{2,1,0:T(8,128)}, f32[2,224,1920]{2,1,0:T(8,128)}, u32[]{:S(2)}, u32[]{:S(2)}) collective-permute-start(f32[2,224,1920]{2,1,0:T(8,128)} %get-tuple-element.117), channel_id=1, source_target_pairs={{0,4},{4,0},{1,5},{5,1},{2,6},{6,2},{3,7},{7,3},{8,12},{12,8},{9,1... | collective-permute-start | bytes 10321928 | tf_op jit(solution)/shard_map/ppermute | solution.py:528
  1510.6 182.9 %collective-permute-start.38 = (f32[1,224,1920]{2,1,0:T(8,128)}, f32[1,224,1920]{2,1,0:T(8,128)}, u32[]{:S(2)}, u32[]{:S(2)}) collective-permute-start(f32[1,224,1920]{2,1,0:T(8,128)} %get-tuple-element.125), channel_id=1, source_target_pairs={{0,4},{4,0},{1,5},{5,1},{2,6},{6,2},{3,7},{7,3},{8,12},{12,8},{9,1... | collective-permute-start | bytes 5160968 | tf_op jit(solution)/shard_map/ppermute | solution.py:528
  1693.5 206.2 %collective-permute-start.34 = (f32[1040,896]{1,0:T(8,128)}, f32[1040,896]{1,0:T(8,128)}, u32[]{:S(2)}, u32[]{:S(2)}) collective-permute-start(f32[1040,896]{1,0:T(8,128)} %combine.15), channel_id=1, source_target_pairs={{0,2},{2,0},{1,3},{3,1},{4,6},{6,4},{5,7},{7,5},{8,10},{10,8},{9,1... | collective-permute-start | bytes 11182088 | tf_op jit(solution)/shard_map/ppermute | solution.py:528
  1701.7 198.1 %collective-permute-start.36 = (f32[1040,896]{1,0:T(8,128)}, f32[1040,896]{1,0:T(8,128)}, u32[]{:S(2)}, u32[]{:S(2)}) collective-permute-start(f32[1040,896]{1,0:T(8,128)} %combine.17), channel_id=1, source_target_pairs={{0,4},{4,0},{1,5},{5,1},{2,6},{6,2},{3,7},{7,3},{8,12},{12,8},{9,1... | collective-permute-start | bytes 11182088 | tf_op jit(solution)/shard_map/ppermute | solution.py:528
  1714.1 197.2 %collective-permute-start.30 = (f32[1040,896]{1,0:T(8,128)}, f32[1040,896]{1,0:T(8,128)}, u32[]{:S(2)}, u32[]{:S(2)}) collective-permute-start(f32[1040,896]{1,0:T(8,128)} %combine.11), channel_id=1, source_target_pairs={{0,2},{2,0},{1,3},{3,1},{4,6},{6,4},{5,7},{7,5},{8,10},{10,8},{9,1... | collective-permute-start | bytes 11182088 | tf_op jit(solution)/shard_map/ppermute | solution.py:528
  1714.9 196.4 %collective-permute-start.32 = (f32[1040,896]{1,0:T(8,128)}, f32[1040,896]{1,0:T(8,128)}, u32[]{:S(2)}, u32[]{:S(2)}) collective-permute-start(f32[1040,896]{1,0:T(8,128)} %combine.13), channel_id=1, source_target_pairs={{0,4},{4,0},{1,5},{5,1},{2,6},{6,2},{3,7},{7,3},{8,12},{12,8},{9,1... | collective-permute-start | bytes 11182088 | tf_op jit(solution)/shard_map/ppermute | solution.py:528
  1733.2 165.3 %collective-permute-start.46 = (f32[1,224,1920]{2,1,0:T(8,128)S(1)}, f32[1,224,1920]{2,1,0:T(8,128)S(1)}, u32[]{:S(2)}, u32[]{:S(2)}) collective-permute-start(f32[1,224,1920]{2,1,0:T(8,128)S(1)} %get-tuple-element.123), channel_id=1, source_target_pairs={{0,4},{4,0},{1,5},{5,1},{2,6},{6,2},{3,7},{7,3},{8,12},{12,8},{9,1... | collective-permute-start | bytes 5160968 | tf_op jit(solution)/shard_map/ppermute | solution.py:528
  (25 other events, 705.5 us)
where the time goes:
time: 1930 us; the launch traced here: 1920 us
  waiting for transfers between devices  1180 us (61%)
  Pallas kernels  576 us (30%)
  starting transfers between devices  73.8 us (4%)
  local copies, waits for them, and re-layouts  51.9 us (3%)
  other arithmetic  42.1 us (2%)
    ppermute x47, waiting for transfers between devices, swap(): return lax.ppermute(value, axis, SWAP)  1180 us
    pallas_call x10, Pallas kernels, run_experts(): pl.pallas_call(functools.partial(expert_kernel, add_into, STARTS[k], n),...  325 us
    pallas_call x10, Pallas kernels, combine(): pl.pallas_call(functools.partial(combine_kernel, base, steps, len(extra),...  129 us
    pallas_call x3, Pallas kernels, gather_rows(): pl.pallas_call(functools.partial(gather_kernel, lo, n), grid=(SRC,), out_...  107 us
    ppermute x47, starting transfers between devices, swap(): return lax.ppermute(value, axis, SWAP)  73.8 us
  transfers between devices with their start and end apart: 47, of which 14 were waited for; matrix products, arithmetic and copies ran while one was open for 5% of the time, Pallas kernels for 29%

commit v1 on v0

--- a/solution.py
+++ b/solution.py
@@ -15,6 +15,7 @@
 F = 640
 CAP = 160
 SRC = 8
+PAIRS = SRC // 2
 EXP = 8
 QUARTER = D // 4
 HALF = D // 2
@@ -89,10 +90,10 @@
 
 
 def routing_kernel(first_ref, *refs):
-    tables = refs[:SRC]
-    pos_ref, gsel_ref, ids_ref, cnt_ref, member = refs[SRC:]
+    tables = refs[:2]
+    pos_ref, gsel_ref, ids_ref, cnt_ref, member = refs[2:]
     first = first_ref[0]
-    for src in range(SRC):
+    for src in range(2):
         block = tables[src][...].astype(F32)
         table = jnp.concatenate([block[:32], block[32:, :TOK - D]], axis=1)
         ids = table[:8].astype(jnp.int32)
@@ -108,74 +109,78 @@
     count = jnp.dot(chosen.astype(BF16), jnp.where(earlier, 1.0, 0.0).astype(BF16), preferred_element_type=F32)
     kept = (chosen > 0.5) & (count < CAP - 0.5)
     slot = jnp.where(kept, count, -1.0).astype(jnp.int32)
-    pos_ref[...] = slot.reshape(SRC, EXP, TOK)
+    pos_ref[...] = slot.reshape(2, EXP, TOK)
     load = lax.dot_general(jnp.ones((8, TOK), BF16), chosen.astype(BF16), (((1,), (1,)), ((), ())), preferred_element_type=F32)
     rows = jnp.minimum(load, float(CAP)).astype(jnp.int32)
     cnt_ref[...] = ((rows + (GRAIN - 1)) >> 4) << 4
 
 
 def routing(first, tokens):
-    shape = (SRC, EXP, TOK)
+    shape = (2, EXP, TOK)
     table = pl.BlockSpec((TABLE_ROWS, D), lambda i: (2 * TOK // TABLE_ROWS, 0))
     whole = pl.BlockSpec(shape, lambda i: (0, 0, 0))
     return pl.pallas_call(
         routing_kernel,
         grid=(1,),
-        out_shape=(jax.ShapeDtypeStruct(shape, jnp.int32), jax.ShapeDtypeStruct(shape, F32), jax.ShapeDtypeStruct(shape, jnp.int32), jax.ShapeDtypeStruct((8, SRC * EXP), jnp.int32)),
-        in_specs=[pl.BlockSpec(memory_space=pltpu.SMEM)] + [table] * SRC,
-        out_specs=(whole, whole, whole, pl.BlockSpec((8, SRC * EXP), lambda i: (0, 0))),
-        scratch_shapes=[pltpu.VMEM((SRC * EXP, TOK), F32)],
+        out_shape=(jax.ShapeDtypeStruct(shape, jnp.int32), jax.ShapeDtypeStruct(shape, F32), jax.ShapeDtypeStruct(shape, jnp.int32), jax.ShapeDtypeStruct((8, 2 * EXP), jnp.int32)),
+        in_specs=[pl.BlockSpec(memory_space=pltpu.SMEM)] + [table] * 2,
+        out_specs=(whole, whole, whole, pl.BlockSpec((8, 2 * EXP), lambda i: (0, 0))),
+        scratch_shapes=[pltpu.VMEM((2 * EXP, TOK), F32)],
         compiler_params=params(),
         name="routing",
-        cost_estimate=pl.CostEstimate(flops=2 * 64 * TOK * TOK, bytes_accessed=3 << 20, transcendentals=0),
+        cost_estimate=pl.CostEstimate(flops=2 * 16 * TOK * TOK, bytes_accessed=1 << 20, transcendentals=0),
     )(first, *tokens)
+
+
+def count_at(cnt_refs, src, e):
+    return cnt_refs[src // 2][0, (src % 2) * EXP + e]
 
 
 def aligned(value):
     return pl.multiple_of(value, GRAIN)
 
 
-def gather_kernel(lo, n, cnt_ref, *refs):
-    tok_refs = refs[:SRC]
-    pos_ref, gate_ref = refs[SRC:SRC + 2]
-    out_refs = refs[SRC + 2:SRC + 5]
-    pick, gcol, buf, stage, offset, sem, out_sem = refs[SRC + 5:]
+def gather_kernel(pair, *refs):
+    cnt_refs = refs[:pair + 1]
+    refs = refs[pair + 1:]
+    tok_refs = refs[:2]
+    pos_ref, gate_ref = refs[2:4]
+    refs = refs[4 + (3 if pair else 0):]
+    out_refs = refs[:3]
+    pick, gcol, buf, stage, offset, sem, out_sem = refs[3:]
     s = pl.program_id(0)
-    slot = lax.rem(s, 2)
 
     def fetch(src):
-        return pltpu.make_async_copy(tok_refs[src].at[pl.ds(0, 2 * TOK), :], buf.at[src % 2], sem.at[src % 2])
-
-    def store(which, j, side, start, place):
+        return pltpu.make_async_copy(tok_refs[src].at[pl.ds(0, 2 * TOK), :], buf.at[src], sem.at[src])
+
+    def store(which, e, side, start, place):
         return pltpu.make_async_copy(
-            stage.at[side, which, pl.ds(aligned(start), CAP), :], out_refs[which].at[j, pl.ds(aligned(place), CAP), :], out_sem.at[side]
+            stage.at[side, which, pl.ds(aligned(start), CAP), :], out_refs[which].at[e, pl.ds(aligned(place), CAP), :], out_sem.at[side]
         )
 
     @pl.when(s == 0)
     def _():
         fetch(0).start()
-        for j in range(n):
-            offset[j] = 0
-
-    for src in range(1, SRC):
-        @pl.when(s == src - 1)
-        def _(src=src):
-            fetch(src).start()
+        fetch(1).start()
+        for e in range(EXP):
+            place = jnp.int32(0)
+            for src in range(2 * pair):
+                place = place + count_at(cnt_refs, src, e)
+            offset[e] = place
 
     slots = lax.broadcasted_iota(jnp.int32, (CAP, TOK), 0)
     starts = []
     total = jnp.int32(0)
-    for j in range(n):
-        e = lo + j
+    for e in range(EXP):
         rows = pl.ds(aligned(total), CAP)
         hit = slots == pos_ref[e:e + 1, :]
         pick[rows, :] = jnp.where(hit, 1.0, 0.0).astype(BF16)
         col = jnp.sum(jnp.where(hit, gate_ref[e:e + 1, :], 0.0), axis=1, keepdims=True)
         gcol[rows, :] = jnp.broadcast_to(col, (CAP, 128))
         starts.append(total)
-        total = total + cnt_ref[0, s * EXP + e]
-
-    for src in range(SRC):
+        total = total + cnt_refs[pair][0, s * EXP + e]
+
+    for src in range(2):
         @pl.when(s == src)
         def _(src=src):
             fetch(src).wait()
@@ -183,61 +188,68 @@
     def body(t, carry):
         rows = pl.ds(pl.multiple_of(t * TILE, TILE), TILE)
         sel = pick[rows, :]
-        x_rows = jnp.dot(sel, buf[slot, :TOK, :], preferred_element_type=F32)
-        stage[slot, 0, rows, :] = x_rows.astype(BF16)
-        dy_rows = jnp.dot(sel, buf[slot, TOK:, :], preferred_element_type=F32)
-        stage[slot, 1, rows, :] = dy_rows.astype(BF16)
-        stage[slot, 2, rows, :] = (gcol[rows, :1] * dy_rows).astype(BF16)
+        x_rows = jnp.dot(sel, buf[s, :TOK, :], preferred_element_type=F32)
+        stage[s, 0, rows, :] = x_rows.astype(BF16)
+        dy_rows = jnp.dot(sel, buf[s, TOK:, :], preferred_element_type=F32)
+        stage[s, 1, rows, :] = dy_rows.astype(BF16)
+        stage[s, 2, rows, :] = (gcol[rows, :1] * dy_rows).astype(BF16)
         return carry
 
     lax.fori_loop(0, (total + (TILE - 1)) // TILE, body, 0)
 
     @pl.when(s > 0)
     def _():
-        for j in range(n):
+        for e in range(EXP):
             for which in range(3):
-                store(which, j, 1 - slot, 0, 0).wait()
-
-    for j in range(n):
-        place = offset[j]
+                store(which, e, 0, 0, 0).wait()
+
+    for e in range(EXP):
+        place = offset[e]
         for which in range(3):
-            store(which, j, slot, starts[j], place).start()
-        offset[j] = place + cnt_ref[0, s * EXP + lo + j]
-
-    @pl.when(s == SRC - 1)
-    def _():
-        for j in range(n):
+            store(which, e, s, starts[e], place).start()
+        offset[e] = place + cnt_refs[pair][0, s * EXP + e]
+
+    @pl.when(s == 1)
+    def _():
+        for e in range(EXP):
             for which in range(3):
-                store(which, j, slot, 0, 0).wait()
-
-
-def gather_rows(counts, tokens, pos, gate, lo, n):
-    rows = jax.ShapeDtypeStruct((n, ROWS, D), BF16)
+                store(which, e, 1, 0, 0).wait()
+
+
+def gather_rows(tables, tokens, rows, pair):
+    shape = jax.ShapeDtypeStruct((EXP, ROWS, D), BF16)
+    pos, gate = tables[pair][:2]
+    counts = [table[3] for table in tables[:pair + 1]]
     table = pl.BlockSpec((None, EXP, TOK), lambda s: (s, 0, 0))
     anywhere = pl.BlockSpec(memory_space=pl.ANY)
-    picked = (n * CAP + TILE - 1) // TILE * TILE
+    given = [] if rows is None else list(rows)
+    operands = [*counts, *tokens[2 * pair:2 * pair + 2], pos, gate, *given]
     return pl.pallas_call(
-        functools.partial(gather_kernel, lo, n),
-        grid=(SRC,),
-        out_shape=(rows, rows, rows),
-        in_specs=[pl.BlockSpec(memory_space=pltpu.SMEM)] + [anywhere] * SRC + [table, table],
+        functools.partial(gather_kernel, pair),
+        grid=(2,),
+        out_shape=(shape, shape, shape),
+        in_specs=[pl.BlockSpec(memory_space=pltpu.SMEM)] * (pair + 1) + [anywhere] * 2 + [table, table] + [anywhere] * len(given),
         out_specs=(anywhere, anywhere, anywhere),
+        input_output_aliases={len(operands) - 3 + i: i for i in range(3)} if given else {},
         scratch_shapes=[
-            pltpu.VMEM((picked, TOK), BF16),
-            pltpu.VMEM((picked, 128), F32),
+            pltpu.VMEM((ROWS, TOK), BF16),
+            pltpu.VMEM((ROWS, 128), F32),
             pltpu.VMEM((2, 2 * TOK, D), BF16),
-            pltpu.VMEM((2, 3, picked, D), BF16),
-            pltpu.SMEM((n,), jnp.int32),
+            pltpu.VMEM((2, 3, ROWS, D), BF16),
+            pltpu.SMEM((EXP,), jnp.int32),
             pltpu.SemaphoreType.DMA((2,)),
             pltpu.SemaphoreType.DMA((2,)),
         ],
         compiler_params=params(),
         name="gather_rows",
-        cost_estimate=pl.CostEstimate(flops=4 * SRC * n * CAP * TOK * D, bytes_accessed=(30 + 7 * n) << 20, transcendentals=0),
-    )(counts, *tokens, pos, gate)
-
-
-def expert_kernel(add_into, lo, n, place_ref, cnt_ref, x_ref, dy_ref, g_ref, own_ref, yr_ref, zo_ref, zf_ref, *refs):
+        cost_estimate=pl.CostEstimate(flops=8 * ROWS * TOK * D, bytes_accessed=20 << 20, transcendentals=0),
+    )(*operands)
+
+
+def expert_kernel(add_into, lo, n, place_ref, *refs):
+    cnt_refs = refs[:PAIRS]
+    x_ref, dy_ref, g_ref, own_ref, yr_ref, zo_ref, zf_ref = refs[PAIRS:PAIRS + 7]
+    refs = refs[PAIRS + 7:]
     if add_into:
         acc_ref, dx_ref, dg_ref, keep_ref, send_ref = refs[:5]
         refs = refs[5:]
@@ -277,9 +289,9 @@
         if add_into:
             acc_copy(0).start()
 
-    count = cnt_ref[0, lo + i]
+    count = count_at(cnt_refs, 0, lo + i)
     for src in range(1, SRC):
-        count = count + cnt_ref[0, src * EXP + lo + i]
+        count = count + count_at(cnt_refs, src, lo + i)
 
     if not add_into:
         dw[...] = jnp.zeros((D, WIDE), F32)
@@ -341,10 +353,10 @@
             copy.wait()
 
 
-def run_experts(place, counts, rows, offset, pieces, acc, k):
+def run_experts(place, counts, rows, pieces, acc, k):
     add_into = acc is not None
     n = CHUNKS[k]
-    row_in = pl.BlockSpec((None, ROWS, D), lambda i: (offset + i, 0, 0))
+    row_in = pl.BlockSpec((None, ROWS, D), lambda i: (STARTS[k] + i, 0, 0))
     anywhere = pl.BlockSpec(memory_space=pl.ANY)
     dx_out = pl.BlockSpec((None, ROWS, D), lambda i: (i, 0, 0))
     dg_out = pl.BlockSpec((None, ROWS, 128), lambda i: (i, 0, 0))
@@ -356,13 +368,13 @@
     else:
         outs += [jax.ShapeDtypeStruct((n, D, WIDE), F32)]
         out_specs += [anywhere]
-    operands = [place, counts, *rows, *pieces] + ([acc] if add_into else [])
+    operands = [place, *counts, *rows, *pieces] + ([acc] if add_into else [])
     smem = pl.BlockSpec(memory_space=pltpu.SMEM)
     return pl.pallas_call(
         functools.partial(expert_kernel, add_into, STARTS[k], n),
         grid=(n,),
         out_shape=tuple(outs),
-        in_specs=[smem, smem] + [row_in] * 3 + [anywhere] * (4 + add_into),
+        in_specs=[smem] * (1 + PAIRS) + [row_in] * 3 + [anywhere] * (4 + add_into),
         out_specs=tuple(out_specs),
         scratch_shapes=[
             pltpu.VMEM((n, D, WIDE), BF16),
@@ -377,13 +389,16 @@
     )(*operands)
 
 
-def combine_kernel(base, steps, extras, final, first_ref, cnt_ref, *refs):
+def combine_kernel(base, steps, extras, final, first_ref, *refs):
+    cnt_refs = refs[:PAIRS]
+    refs = refs[PAIRS:]
     dx_refs = refs[:N_CHUNK]
     dg_refs = refs[N_CHUNK:2 * N_CHUNK]
     refs = refs[2 * N_CHUNK:]
-    pos_ref, ids_ref = refs[:2]
-    extra_refs = refs[2:2 + extras]
-    refs = refs[2 + extras:]
+    pos_refs = refs[:steps]
+    id_refs = refs[steps:2 * steps]
+    extra_refs = refs[2 * steps:2 * steps + extras]
+    refs = refs[2 * steps + extras:]
     if final == 2:
         refs = refs[2:]
     if final:
@@ -405,7 +420,7 @@
                 e = STARTS[k] + j
                 place = jnp.int32(0)
                 for src in range(SRC - 1):
-                    place = place + jnp.where(src < source, cnt_ref[0, src * EXP + e], 0)
+                    place = place + jnp.where(src < source, count_at(cnt_refs, src, e), 0)
                 window = pl.ds(aligned(place), CAP)
                 out.append(pltpu.make_async_copy(dx_refs[k].at[j, window, :], stage.at[lax.rem(i, 2), e], sem.at[lax.rem(i, 2)]))
                 out.append(pltpu.make_async_copy(dg_refs[k].at[j, window, :], dg_stage.at[lax.rem(i, 2), e], sem.at[lax.rem(i, 2)]))
@@ -422,20 +437,26 @@
         for load in loads(step + 1):
             load.start()
 
-    source = base + 2 * step
+    pos = pos_refs[0][...]
+    ids = id_refs[0][...]
+    for i in range(1, steps):
+        pos = jnp.where(step == i, pos_refs[i][...], pos)
+        ids = jnp.where(step == i, id_refs[i][...], ids)
     slots = lax.broadcasted_iota(jnp.int32, (CAP, TOK), 0)
     total = jnp.int32(0)
     starts, counts = [], []
     for e in range(EXP):
-        pick[pl.ds(aligned(total), CAP), :] = jnp.where(slots == pos_ref[e:e + 1, :], 1.0, 0.0).astype(BF16)
+        pick[pl.ds(aligned(total), CAP), :] = jnp.where(slots == pos[e:e + 1, :], 1.0, 0.0).astype(BF16)
         starts.append(total)
-        counts.append(cnt_ref[0, source * EXP + e])
+        here = count_at(cnt_refs, base, e)
+        for i in range(1, steps):
+            here = jnp.where(step == i, count_at(cnt_refs, base + 2 * i, e), here)
+        counts.append(here)
         total = total + counts[e]
     pick[pl.ds(aligned(total), TILE), :] = jnp.zeros((TILE, TOK), BF16)
 
     for load in loads(step):
         load.wait()
-    ids = ids_ref[...]
     dg_choice = jnp.zeros((TOP_K, TOK), F32)
     for e in range(EXP):
         block = stage[side, e]
@@ -443,7 +464,7 @@
             live = lax.broadcasted_iota(jnp.int32, (CAP, 1), 0) < counts[e]
             block = jnp.where(live, block.astype(F32), 0.0).astype(BF16)
         rows[pl.ds(aligned(starts[e]), CAP), :] = block
-        hit = slots == pos_ref[e:e + 1, :]
+        hit = slots == pos[e:e + 1, :]
         dg_tok = jnp.sum(jnp.where(hit, dg_stage[side, e, :, :1], 0.0), axis=0, keepdims=True)
         dg_choice = dg_choice + jnp.where(ids == first + e, dg_tok, 0.0)
 
@@ -472,11 +493,11 @@
         sums[TOK + 8:, :TOK - D] = right
 
 
-def combine(first, table, dx_rows, dg_rows, base, steps, partner=None, arrived=(), final=None, mb=0):
-    pos, ids, counts = table
+def combine(first, tables, dx_rows, dg_rows, base, steps, partner=None, arrived=(), final=None, mb=0):
     smem = pl.BlockSpec(memory_space=pltpu.SMEM)
     anywhere = pl.BlockSpec(memory_space=pl.ANY)
-    block = pl.BlockSpec((None, EXP, TOK), lambda i: (base + 2 * i, 0, 0))
+    block = pl.BlockSpec((None, EXP, TOK), lambda i: (base % 2, 0, 0))
+    used = tables[base // 2:base // 2 + steps]
     whole = pl.BlockSpec((SUM_ROWS, D), lambda i: (0, 0))
     extra_specs = [] if partner is None else [pl.BlockSpec((None, SUM_ROWS, D), lambda i: (base // 2, 0, 0))]
     extra_specs += [whole] * len(arrived)
@@ -488,8 +509,8 @@
         pltpu.VMEM((2, EXP, CAP, 128), F32),
         pltpu.SemaphoreType.DMA((2,)),
     ]
-    in_specs = [smem, smem] + [anywhere] * (2 * N_CHUNK) + [block, block] + extra_specs
-    operands = [first, counts, *dx_rows, *dg_rows, pos, ids, *extra]
+    in_specs = [smem] * (1 + PAIRS) + [anywhere] * (2 * N_CHUNK) + [block] * (2 * steps) + extra_specs
+    operands = [first, *(t[3] for t in tables), *dx_rows, *dg_rows, *(t[0] for t in used), *(t[2] for t in used), *extra]
     mode, aliases = 0, {}
     if final is None:
         if steps > 1:
@@ -540,8 +561,8 @@
         from_xy = swap(from_y, 'x')
         return [
             block, swap(block, 'c'),
+            from_y, swap(from_y, 'c'),
             from_x, swap(from_x, 'c'),
-            from_y, swap(from_y, 'c'),
             from_xy, swap(from_xy, 'c'),
         ]
 
@@ -568,27 +589,24 @@
             from_yz = swap(from_y, 'z')
             pieces.append((own, from_y, from_z, from_yz))
 
-        tables = [routing(first, tokens[mb]) for mb in range(MICRO)]
-        split = STARTS[2]
-
-        def gather(mb, lo, n):
-            pos, gate_sel, _, counts = tables[mb]
-            return gather_rows(counts, tokens[mb], pos, gate_sel, lo, n)
-
-        whole = gather(0, 0, EXP)
-        head = gather(1, 0, split)
-        tail = gather(1, split, EXP - split)
+        tables, rows = [], []
+        for mb in range(MICRO):
+            tables.append([routing(first, tokens[mb][2 * p:2 * p + 2]) for p in range(PAIRS)])
+            got = None
+            for p in range(PAIRS):
+                got = gather_rows(tables[mb], tokens[mb], got, p)
+            rows.append(got)
+        counts = [[table[3] for table in tables[mb]] for mb in range(MICRO)]
 
         acc, keep, send = [], [], []
         dx_rows, dg_rows = ([], []), ([], [])
         for k in range(N_CHUNK):
-            res = run_experts(place, tables[0][3], whole, STARTS[k], pieces[k], None, k)
+            res = run_experts(place, counts[0], rows[0], pieces[k], None, k)
             dx_rows[0].append(res[0])
             dg_rows[0].append(res[1])
             acc.append(res[2])
         for k in range(N_CHUNK):
-            rows, offset = (head, STARTS[k]) if STARTS[k] < split else (tail, STARTS[k] - split)
-            res = run_experts(place, tables[1][3], rows, offset, pieces[k], acc[k], k)
+            res = run_experts(place, counts[1], rows[1], pieces[k], acc[k], k)
             dx_rows[1].append(res[0])
             dg_rows[1].append(res[1])
             keep.append(res[2])
@@ -596,12 +614,11 @@
 
         done = ()
         for mb in range(MICRO):
-            pos, _, id_table, counts = tables[mb]
-            args = (first, (pos, id_table, counts), dx_rows[mb], dg_rows[mb])
+            args = (first, tables[mb], dx_rows[mb], dg_rows[mb])
             partner = swap(combine(*args, 1, 4), 'c')
             far = swap(combine(*args, 6, 1, partner), 'x')
-            near = swap(combine(*args, 2, 1, partner), 'x')
-            last = swap(combine(*args, 4, 1, partner, (far,)), 'y')
+            near = swap(combine(*args, 4, 1, partner), 'x')
+            last = swap(combine(*args, 2, 1, partner, (far,)), 'y')
             done = combine(*args, 0, 1, partner, (near, last), final=done, mb=mb)
 
         bufs = [jnp.zeros((2 * EXP, QUARTER, F), F32)] * 3

time: 1930 us -> 1890 us (0.979)
  waiting for transfers between devices: 1180 us -> 1130 us
  Pallas kernels: 576 us -> 612 us
    ppermute x47, waiting for transfers between devices: 1180 us -> 1130 us  [swap(): return lax.ppermute(value, axis, SWAP)]
    pallas_call x3 -> x8, Pallas kernels: 107 us -> 130 us  [gather_rows(): pl.pallas_call(functools.partial(gather_kernel, pair), grid=(2,), out_sha...]
  transfers between devices with their start and end apart: 47 -> 47, of which waited for: 14 -> 15; matrix products, arithmetic and copies ran while one was open for 5% -> 4% of each run, Pallas kernels for 29% -> 32%
where the time goes in v1:
time: 1890 us; the launch traced here: 1880 us
  waiting for transfers between devices  1130 us (60%)
  Pallas kernels  612 us (32%)
  starting transfers between devices  55.8 us (3%)
  local copies, waits for them, and re-layouts  43 us (2%)
  other arithmetic  41.7 us (2%)
    ppermute x47, waiting for transfers between devices, swap(): return lax.ppermute(value, axis, SWAP)  1130 us
    pallas_call x10, Pallas kernels, run_experts(): pl.pallas_call(functools.partial(expert_kernel, add_into, STARTS[k], n),...  325 us
    pallas_call x10, Pallas kernels, combine(): pl.pallas_call(functools.partial(combine_kernel, base, steps, len(extra),...  130 us
    pallas_call x8, Pallas kernels, gather_rows(): pl.pallas_call(functools.partial(gather_kernel, pair), grid=(2,), out_sha...  130 us
    ppermute x47, starting transfers between devices, swap(): return lax.ppermute(value, axis, SWAP)  55.8 us
  transfers between devices with their start and end apart: 47, of which 15 were waited for; matrix products, arithmetic and copies ran while one was open for 4% of the time, Pallas kernels for 32%

profile of v1, /device:TPU:0, one launch (start us, length us, event | category | flops | bytes accessed | tf_op | source)
XLA Modules:
  0.0 1883.3 jit_solution(17722769183560887855)
XLA Ops:
  14.7 76.1 %collective-permute-done.11.refs_0_.refs_2_ = bf16[2112,896]{1,0:T(8,128)(2,1)} collective-permute-done((bf16[2112,896]{1,0:T(8,128)(2,1)}, bf16[2112,896]{1,0:T(8,128)(2,1)}, u32[]{:S(2)}, u32[]{:S(2)}) %collective-permute-start.11) | collective-permute-done | bytes 3784736 | tf_op jit(solution)/shard_map/ppermute | solution.py:549
  99.9 71.8 %collective-permute-done.1.refs_0_.refs_2_ = bf16[2112,896]{1,0:T(8,128)(2,1)} collective-permute-done((bf16[2112,896]{1,0:T(8,128)(2,1)}, bf16[2112,896]{1,0:T(8,128)(2,1)}, u32[]{:S(2)}, u32[]{:S(2)}) %collective-permute-start.1) | collective-permute-done | bytes 3784736 | tf_op jit(solution)/shard_map/ppermute | solution.py:549
  188.0 17.0 gather_rows.12
  205.0 49.2 %collective-permute-done.15.refs_0_.refs_4_ = bf16[2112,896]{1,0:T(8,128)(2,1)} collective-permute-done((bf16[2112,896]{1,0:T(8,128)(2,1)}, bf16[2112,896]{1,0:T(8,128)(2,1)}, u32[]{:S(2)}, u32[]{:S(2)}) %collective-permute-start.15) | collective-permute-done | bytes 3784736 | tf_op jit(solution)/shard_map/ppermute | solution.py:549
  254.3 14.2 gather_rows.8
  273.2 5.6 collective-permute-start.24
  284.9 15.8 gather_rows.13
  300.7 17.2 gather_rows.14
  317.9 16.4 gather_rows.9
  334.3 14.6 gather_rows.10
  351.3 18.0 gather_rows.15
  371.4 38.1 %experts_first.8 = (bf16[2,1280,896]{2,1,0:T(8,128)(2,1)}, f32[2,1280,128]{2,1,0:T(8,128)}, f32[2,896,1920]{2,1,0:T(8,128)}) custom-call(s32[2]{0:T(128)} %pad_add_fusion.place_ref, s32[8,16]{1,0:T(8,128)} %get-tuple-element.124.refs_0_, s32[8,16]{1,0:T(8,128)} %get-tuple-element.125.refs_1_, s32[8,16]{1,0:T(8,128)} %get-tuple-element.126.refs_2_, ...), custom_call_target="tpu_custom_call" | custom-call | flops 26424115200 | bytes 50331648 | tf_op jit(solution)/shard_map/experts_first/pallas_call | solution.py:373
  411.6 35.3 %collective-permute-done.22.refs_10_ = bf16[2,224,1920]{2,1,0:T(8,128)(2,1)} collective-permute-done((bf16[2,224,1920]{2,1,0:T(8,128)(2,1)}, bf16[2,224,1920]{2,1,0:T(8,128)(2,1)}, u32[]{:S(2)}, u32[]{:S(2)}) %collective-permute-start.22) | collective-permute-done | bytes 1720352 | tf_op jit(solution)/shard_map/ppermute | solution.py:549
  447.6 34.8 %experts_first.7 = (bf16[2,1280,896]{2,1,0:T(8,128)(2,1)}, f32[2,1280,128]{2,1,0:T(8,128)}, f32[2,896,1920]{2,1,0:T(8,128)}) custom-call(s32[2]{0:T(128)} %pad_add_fusion.place_ref, s32[8,16]{1,0:T(8,128)} %get-tuple-element.124.refs_0_, s32[8,16]{1,0:T(8,128)} %get-tuple-element.125.refs_1_, s32[8,16]{1,0:T(8,128)} %get-tuple-element.126.refs_2_, ...), custom_call_target="tpu_custom_call" | custom-call | flops 26424115200 | bytes 50331648 | tf_op jit(solution)/shard_map/experts_first/pallas_call | solution.py:373
  488.3 20.0 %experts_first.9 = (bf16[1,1280,896]{2,1,0:T(8,128)(2,1)}, f32[1,1280,128]{2,1,0:T(8,128)}, f32[1,896,1920]{2,1,0:T(8,128)}) custom-call(s32[2]{0:T(128)} %pad_add_fusion.place_ref, s32[8,16]{1,0:T(8,128)} %get-tuple-element.124.refs_0_, s32[8,16]{1,0:T(8,128)} %get-tuple-element.125.refs_1_, s32[8,16]{1,0:T(8,128)} %get-tuple-element.126.refs_2_, ...), custom_call_target="tpu_custom_call" | custom-call | flops 13212057600 | bytes 25165824 | tf_op jit(solution)/shard_map/experts_first/pallas_call | solution.py:373
  508.3 31.2 %collective-permute-done.8.refs_9_ = bf16[1,224,1920]{2,1,0:T(8,128)(2,1)S(1)} collective-permute-done((bf16[1,224,1920]{2,1,0:T(8,128)(2,1)S(1)}, bf16[1,224,1920]{2,1,0:T(8,128)(2,1)S(1)}, u32[]{:S(2)}, u32[]{:S(2)}) %collective-permute-start.8) | collective-permute-done | bytes 860192 | tf_op jit(solution)/shard_map/ppermute | solution.py:549
  539.6 18.5 collective-permute-done.9.refs_10_
  558.1 26.5 %experts_first.5 = (bf16[1,1280,896]{2,1,0:T(8,128)(2,1)}, f32[1,1280,128]{2,1,0:T(8,128)}, f32[1,896,1920]{2,1,0:T(8,128)}) custom-call(s32[2]{0:T(128)} %pad_add_fusion.place_ref, s32[8,16]{1,0:T(8,128)} %get-tuple-element.124.refs_0_, s32[8,16]{1,0:T(8,128)} %get-tuple-element.125.refs_1_, s32[8,16]{1,0:T(8,128)} %get-tuple-element.126.refs_2_, ...), custom_call_target="tpu_custom_call" | custom-call | flops 13212057600 | bytes 25165824 | tf_op jit(solution)/shard_map/experts_first/pallas_call | solution.py:373
  584.6 10.4 collective-permute-done.19.refs_10_
  595.0 41.3 %experts_first.6 = (bf16[2,1280,896]{2,1,0:T(8,128)(2,1)}, f32[2,1280,128]{2,1,0:T(8,128)}, f32[2,896,1920]{2,1,0:T(8,128)}) custom-call(s32[2]{0:T(128)} %pad_add_fusion.place_ref, s32[8,16]{1,0:T(8,128)} %get-tuple-element.124.refs_0_, s32[8,16]{1,0:T(8,128)} %get-tuple-element.125.refs_1_, s32[8,16]{1,0:T(8,128)} %get-tuple-element.126.refs_2_, ...), custom_call_target="tpu_custom_call" | custom-call | flops 26424115200 | bytes 50331648 | tf_op jit(solution)/shard_map/experts_first/pallas_call | solution.py:373
  636.3 23.9 %combine.14 = f32[4,1040,896]{2,1,0:T(8,128)} custom-call(s32[1]{0:T(128)} %bitcast.first_ref, s32[8,16]{1,0:T(8,128)} %get-tuple-element.124.refs_0_, s32[8,16]{1,0:T(8,128)} %get-tuple-element.125.refs_1_, s32[8,16]{1,0:T(8,128)} %get-tuple-element.126.refs_2_, s32[8,16]{1,0:T(8,128)} %get-tuple-element.127.refs_3_, ...), custom_call_target="tpu_custom_call" | custom-call | flops 9395240960 | bytes 33554432 | tf_op jit(solution)/shard_map/combine/pallas_call | solution.py:531
  662.5 16.8 gather_rows.11
  679.4 21.7 %experts_second.9 = (bf16[1,1280,896]{2,1,0:T(8,128)(2,1)}, f32[1,1280,128]{2,1,0:T(8,128)}, f32[1,448,1920]{2,1,0:T(8,128)}, f32[1,448,1920]{2,1,0:T(8,128)}) custom-call(s32[2]{0:T(128)} %pad_add_fusion.place_ref, s32[8,16]{1,0:T(8,128)} %get-tuple-element.100.refs_0_, s32[8,16]{1,0:T(8,128)} %get-tuple-element.101.refs_1_, ...), custom_call_target="tpu_custom_call" | custom-call | flops 13212057600 | bytes 25165824 | tf_op jit(solution)/shard_map/experts_second/pallas_call | solution.py:373
  701.1 40.1 %experts_second.8 = (bf16[2,1280,896]{2,1,0:T(8,128)(2,1)}, f32[2,1280,128]{2,1,0:T(8,128)}, f32[2,448,1920]{2,1,0:T(8,128)}, f32[2,448,1920]{2,1,0:T(8,128)}) custom-call(s32[2]{0:T(128)} %pad_add_fusion.place_ref, s32[8,16]{1,0:T(8,128)} %get-tuple-element.100.refs_0_, s32[8,16]{1,0:T(8,128)} %get-tuple-element.101.refs_1_, ...), custom_call_target="tpu_custom_call" | custom-call | flops 26424115200 | bytes 50331648 | tf_op jit(solution)/shard_map/experts_second/pallas_call | solution.py:373
  741.2 40.5 %experts_second.7 = (bf16[2,1280,896]{2,1,0:T(8,128)(2,1)}, f32[2,1280,128]{2,1,0:T(8,128)}, f32[2,448,1920]{2,1,0:T(8,128)}, f32[2,448,1920]{2,1,0:T(8,128)}) custom-call(s32[2]{0:T(128)} %pad_add_fusion.place_ref, s32[8,16]{1,0:T(8,128)} %get-tuple-element.100.refs_0_, s32[8,16]{1,0:T(8,128)} %get-tuple-element.101.refs_1_, ...), custom_call_target="tpu_custom_call" | custom-call | flops 26424115200 | bytes 50331648 | tf_op jit(solution)/shard_map/experts_second/pallas_call | solution.py:373
  781.6 40.8 %experts_second.6 = (bf16[2,1280,896]{2,1,0:T(8,128)(2,1)}, f32[2,1280,128]{2,1,0:T(8,128)}, f32[2,448,1920]{2,1,0:T(8,128)}, f32[2,448,1920]{2,1,0:T(8,128)}) custom-call(s32[2]{0:T(128)} %pad_add_fusion.place_ref, s32[8,16]{1,0:T(8,128)} %get-tuple-element.100.refs_0_, s32[8,16]{1,0:T(8,128)} %get-tuple-element.101.refs_1_, ...), custom_call_target="tpu_custom_call" | custom-call | flops 26424115200 | bytes 50331648 | tf_op jit(solution)/shard_map/experts_second/pallas_call | solution.py:373
  822.4 21.8 %experts_second.5 = (bf16[1,1280,896]{2,1,0:T(8,128)(2,1)}, f32[1,1280,128]{2,1,0:T(8,128)}, f32[1,448,1920]{2,1,0:T(8,128)}, f32[1,448,1920]{2,1,0:T(8,128)}) custom-call(s32[2]{0:T(128)} %pad_add_fusion.place_ref, s32[8,16]{1,0:T(8,128)} %get-tuple-element.100.refs_0_, s32[8,16]{1,0:T(8,128)} %get-tuple-element.101.refs_1_, ...), custom_call_target="tpu_custom_call" | custom-call | flops 13212057600 | bytes 25165824 | tf_op jit(solution)/shard_map/experts_second/pallas_call | solution.py:373
  844.2 23.6 %combine.10 = f32[4,1040,896]{2,1,0:T(8,128)} custom-call(s32[1]{0:T(128)} %bitcast.first_ref, s32[8,16]{1,0:T(8,128)} %get-tuple-element.100.refs_0_, s32[8,16]{1,0:T(8,128)} %get-tuple-element.101.refs_1_, s32[8,16]{1,0:T(8,128)} %get-tuple-element.102.refs_2_, s32[8,16]{1,0:T(8,128)} %get-tuple-element.103.refs_3_, ...), custom_call_target="tpu_custom_call" | custom-call | flops 9395240960 | bytes 33554432 | tf_op jit(solution)/shard_map/combine/pallas_call | solution.py:531
  867.8 16.2 collective-permute-start.29
  886.0 149.3 %collective-permute-done.41 = f32[2,448,1920]{2,1,0:T(8,128)} collective-permute-done((f32[2,448,1920]{2,1,0:T(8,128)}, f32[2,448,1920]{2,1,0:T(8,128)}, u32[]{:S(2)}, u32[]{:S(2)}) %collective-permute-start.41) | collective-permute-done | bytes 6881312 | tf_op jit(solution)/shard_map/ppermute | solution.py:549
  1037.3 10.1 combine.16
  1047.4 9.1 combine.12
  1056.5 126.2 %collective-permute-done.39 = f32[2,448,1920]{2,1,0:T(8,128)} collective-permute-done((f32[2,448,1920]{2,1,0:T(8,128)}, f32[2,448,1920]{2,1,0:T(8,128)}, u32[]{:S(2)}, u32[]{:S(2)}) %collective-permute-start.39) | collective-permute-done | bytes 6881312 | tf_op jit(solution)/shard_map/ppermute | solution.py:549
  1182.7 8.5 dynamic-slice_add_fusion.2
  1191.3 8.6 dynamic-slice_add_fusion.4
  1199.9 204.0 %collective-permute-done.45 = f32[1,448,1920]{2,1,0:T(8,128)} collective-permute-done((f32[1,448,1920]{2,1,0:T(8,128)}, f32[1,448,1920]{2,1,0:T(8,128)}, u32[]{:S(2)}, u32[]{:S(2)}) %collective-permute-start.45) | collective-permute-done | bytes 3440672 | tf_op jit(solution)/shard_map/ppermute | solution.py:549
  1406.0 6.7 dynamic-slice_add_fusion
  1412.7 64.0 %collective-permute-done.37 = f32[1,448,1920]{2,1,0:T(8,128)} collective-permute-done((f32[1,448,1920]{2,1,0:T(8,128)}, f32[1,448,1920]{2,1,0:T(8,128)}, u32[]{:S(2)}, u32[]{:S(2)}) %collective-permute-start.37) | collective-permute-done | bytes 3440672 | tf_op jit(solution)/shard_map/ppermute | solution.py:549
  1482.3 4.6 broadcast_in_dim.3.clone.1
  1487.8 11.0 combine.15
  1498.7 9.1 combine.11
  1507.9 11.1 combine.17
  1519.0 144.2 %collective-permute-done.38 = f32[1,224,1920]{2,1,0:T(8,128)} collective-permute-done((f32[1,224,1920]{2,1,0:T(8,128)}, f32[1,224,1920]{2,1,0:T(8,128)}, u32[]{:S(2)}, u32[]{:S(2)}) %collective-permute-start.38) | collective-permute-done | bytes 1720352 | tf_op jit(solution)/shard_map/ppermute | solution.py:549
  1664.8 10.5 combine.13
  1677.8 4.6 broadcast_in_dim.3.clone.2
  1713.2 146.8 %collective-permute-done.46 = f32[1,224,1920]{2,1,0:T(8,128)S(1)} collective-permute-done((f32[1,224,1920]{2,1,0:T(8,128)S(1)}, f32[1,224,1920]{2,1,0:T(8,128)S(1)}, u32[]{:S(2)}, u32[]{:S(2)}) %collective-permute-start.46) | collective-permute-done | bytes 1720352 | tf_op jit(solution)/shard_map/ppermute | solution.py:549
  1861.3 11.2 combine.18
  1872.5 10.5 combine.19
  (152 shorter events, 114.1 us)
Async XLA Ops:
  4.5 9.3 collective-permute-start.10
  5.3 85.5 %collective-permute-start.11 = (bf16[2112,896]{1,0:T(8,128)(2,1)}, bf16[2112,896]{1,0:T(8,128)(2,1)}, u32[]{:S(2)}, u32[]{:S(2)}) collective-permute-start(bf16[2112,896]{1,0:T(8,128)(2,1)} %token_block.3.refs_0_.refs_1_), channel_id=1, source_target_pairs={{0,4},{4,0},{1,5},{5,1},{2,6},{6,2},{3,7},{7,3},{8,12},{12,8},{9,1... | collective-permute-start | bytes 11354120 | tf_op jit(solution)/shard_map/ppermute | solution.py:549
  7.8 87.2 %collective-permute-start.13 = (bf16[2112,896]{1,0:T(8,128)(2,1)}, bf16[2112,896]{1,0:T(8,128)(2,1)}, u32[]{:S(2)}, u32[]{:S(2)}) collective-permute-start(bf16[2112,896]{1,0:T(8,128)(2,1)} %token_block.3.refs_0_.refs_1_), channel_id=1, source_target_pairs={{0,2},{2,0},{1,3},{3,1},{4,6},{6,4},{5,7},{7,5},{8,10},{10,8},{9,1... | collective-permute-start | bytes 11354120 | tf_op jit(solution)/shard_map/ppermute | solution.py:549
  13.2 86.4 %collective-permute-start = (bf16[2112,896]{1,0:T(8,128)(2,1)}, bf16[2112,896]{1,0:T(8,128)(2,1)}, u32[]{:S(2)}, u32[]{:S(2)}) collective-permute-start(bf16[2112,896]{1,0:T(8,128)(2,1)} %token_block.2.refs_0_.refs_1_), channel_id=1, source_target_pairs={{0,1},{1,0},{2,3},{3,2},{4,5},{5,4},{6,7},{7,6},{8,9},{9,8},{10,11... | collective-permute-start | bytes 11354120 | tf_op jit(solution)/shard_map/ppermute | solution.py:549
  13.3 158.4 %collective-permute-start.1 = (bf16[2112,896]{1,0:T(8,128)(2,1)}, bf16[2112,896]{1,0:T(8,128)(2,1)}, u32[]{:S(2)}, u32[]{:S(2)}) collective-permute-start(bf16[2112,896]{1,0:T(8,128)(2,1)} %token_block.2.refs_0_.refs_1_), channel_id=1, source_target_pairs={{0,4},{4,0},{1,5},{5,1},{2,6},{6,2},{3,7},{7,3},{8,12},{12,8},{9,1... | collective-permute-start | bytes 11354120 | tf_op jit(solution)/shard_map/ppermute | solution.py:549
  13.8 160.1 %collective-permute-start.3 = (bf16[2112,896]{1,0:T(8,128)(2,1)}, bf16[2112,896]{1,0:T(8,128)(2,1)}, u32[]{:S(2)}, u32[]{:S(2)}) collective-permute-start(bf16[2112,896]{1,0:T(8,128)(2,1)} %token_block.2.refs_0_.refs_1_), channel_id=1, source_target_pairs={{0,2},{2,0},{1,3},{3,1},{4,6},{6,4},{5,7},{7,5},{8,10},{10,8},{9,1... | collective-permute-start | bytes 11354120 | tf_op jit(solution)/shard_map/ppermute | solution.py:549
  90.8 97.1 %collective-permute-start.12 = (bf16[2112,896]{1,0:T(8,128)(2,1)}, bf16[2112,896]{1,0:T(8,128)(2,1)}, u32[]{:S(2)}, u32[]{:S(2)}) collective-permute-start(bf16[2112,896]{1,0:T(8,128)(2,1)} %collective-permute-done.11.refs_0_.refs_2_), channel_id=1, source_target_pairs={{0,1},{1,0},{2,3},{3,2},{4,5},{5,4},{6,7},{7,6},{8,9},{9,8},{10,11... | collective-permute-start | bytes 11354120 | tf_op jit(solution)/shard_map/ppermute | solution.py:549
  95.1 159.2 %collective-permute-start.15 = (bf16[2112,896]{1,0:T(8,128)(2,1)}, bf16[2112,896]{1,0:T(8,128)(2,1)}, u32[]{:S(2)}, u32[]{:S(2)}) collective-permute-start(bf16[2112,896]{1,0:T(8,128)(2,1)} %collective-permute-done.11.refs_0_.refs_2_), channel_id=1, source_target_pairs={{0,2},{2,0},{1,3},{3,1},{4,6},{6,4},{5,7},{7,5},{8,10},{10,8},{9,1... | collective-permute-start | bytes 11354120 | tf_op jit(solution)/shard_map/ppermute | solution.py:549
  97.5 251.5 %copy-start.4 = (bf16[1,224,1920]{2,1,0:T(8,128)(2,1)}, bf16[1,224,1920]{2,1,0:T(8,128)(2,1)S(1)}, u32[]{:S(2)}) copy-start(bf16[1,224,1920]{2,1,0:T(8,128)(2,1)S(1)} %pad_maximum_fusion.8.refs_7_) | copy-start | bytes 2580484
  99.7 171.0 %collective-permute-start.14 = (bf16[2112,896]{1,0:T(8,128)(2,1)}, bf16[2112,896]{1,0:T(8,128)(2,1)}, u32[]{:S(2)}, u32[]{:S(2)}) collective-permute-start(bf16[2112,896]{1,0:T(8,128)(2,1)} %collective-permute-done.13.refs_0_.refs_3_), channel_id=1, source_target_pairs={{0,1},{1,0},{2,3},{3,2},{4,5},{5,4},{6,7},{7,6},{8,9},{9,8},{10,11... | collective-permute-start | bytes 11354120 | tf_op jit(solution)/shard_map/ppermute | solution.py:549
  171.7 101.5 %collective-permute-start.2 = (bf16[2112,896]{1,0:T(8,128)(2,1)}, bf16[2112,896]{1,0:T(8,128)(2,1)}, u32[]{:S(2)}, u32[]{:S(2)}) collective-permute-start(bf16[2112,896]{1,0:T(8,128)(2,1)} %collective-permute-done.1.refs_0_.refs_2_), channel_id=1, source_target_pairs={{0,1},{1,0},{2,3},{3,2},{4,5},{5,4},{6,7},{7,6},{8,9},{9,8},{10,11... | collective-permute-start | bytes 11354120 | tf_op jit(solution)/shard_map/ppermute | solution.py:549
  173.9 108.7 %collective-permute-start.4 = (bf16[2112,896]{1,0:T(8,128)(2,1)}, bf16[2112,896]{1,0:T(8,128)(2,1)}, u32[]{:S(2)}, u32[]{:S(2)}) collective-permute-start(bf16[2112,896]{1,0:T(8,128)(2,1)} %collective-permute-done.3.refs_0_.refs_3_), channel_id=1, source_target_pairs={{0,1},{1,0},{2,3},{3,2},{4,5},{5,4},{6,7},{7,6},{8,9},{9,8},{10,11... | collective-permute-start | bytes 11354120 | tf_op jit(solution)/shard_map/ppermute | solution.py:549
  187.9 93.1 %collective-permute-start.23 = (bf16[2,224,1920]{2,1,0:T(8,128)(2,1)}, bf16[2,224,1920]{2,1,0:T(8,128)(2,1)}, u32[]{:S(2)}, u32[]{:S(2)}) collective-permute-start(bf16[2,224,1920]{2,1,0:T(8,128)(2,1)} %pad_maximum_fusion.5), channel_id=1, source_target_pairs={{0,4},{4,0},{1,5},{5,1},{2,6},{6,2},{3,7},{7,3},{8,12},{12,8},{9,1... | collective-permute-start | bytes 5160968 | tf_op jit(solution)/shard_map/ppermute | solution.py:549
  254.3 94.7 %collective-permute-start.16 = (bf16[2112,896]{1,0:T(8,128)(2,1)}, bf16[2112,896]{1,0:T(8,128)(2,1)}, u32[]{:S(2)}, u32[]{:S(2)}) collective-permute-start(bf16[2112,896]{1,0:T(8,128)(2,1)} %collective-permute-done.15.refs_0_.refs_4_), channel_id=1, source_target_pairs={{0,1},{1,0},{2,3},{3,2},{4,5},{5,4},{6,7},{7,6},{8,9},{9,8},{10,11... | collective-permute-start | bytes 11354120 | tf_op jit(solution)/shard_map/ppermute | solution.py:549
  270.7 138.8 %collective-permute-start.26 = (bf16[1,224,1920]{2,1,0:T(8,128)(2,1)}, bf16[1,224,1920]{2,1,0:T(8,128)(2,1)}, u32[]{:S(2)}, u32[]{:S(2)}) collective-permute-start(bf16[1,224,1920]{2,1,0:T(8,128)(2,1)} %pad_maximum_fusion.9), channel_id=1, source_target_pairs={{0,4},{4,0},{1,5},{5,1},{2,6},{6,2},{3,7},{7,3},{8,12},{12,8},{9,1... | collective-permute-start | bytes 2580488 | tf_op jit(solution)/shard_map/ppermute | solution.py:549
  273.2 96.1 %collective-permute-start.24 = (bf16[2,224,1920]{2,1,0:T(8,128)(2,1)}, bf16[2,224,1920]{2,1,0:T(8,128)(2,1)}, u32[]{:S(2)}, u32[]{:S(2)}) collective-permute-start(bf16[2,224,1920]{2,1,0:T(8,128)(2,1)} %pad_maximum_fusion.4.refs_7_), channel_id=1, source_target_pairs={{0,8},{8,0},{1,9},{9,1},{2,10},{10,2},{3,11},{11,3},{4,12},{12,4},... | collective-permute-start | bytes 5160968 | tf_op jit(solution)/shard_map/ppermute | solution.py:549
  281.1 89.1 %collective-permute-start.20 = (bf16[2,224,1920]{2,1,0:T(8,128)(2,1)}, bf16[2,224,1920]{2,1,0:T(8,128)(2,1)}, u32[]{:S(2)}, u32[]{:S(2)}) collective-permute-start(bf16[2,224,1920]{2,1,0:T(8,128)(2,1)} %pad_maximum_fusion.3), channel_id=1, source_target_pairs={{0,4},{4,0},{1,5},{5,1},{2,6},{6,2},{3,7},{7,3},{8,12},{12,8},{9,1... | collective-permute-start | bytes 5160968 | tf_op jit(solution)/shard_map/ppermute | solution.py:549
  282.6 88.8 %collective-permute-start.25 = (bf16[2,224,1920]{2,1,0:T(8,128)(2,1)}, bf16[2,224,1920]{2,1,0:T(8,128)(2,1)}, u32[]{:S(2)}, u32[]{:S(2)}) collective-permute-start(bf16[2,224,1920]{2,1,0:T(8,128)(2,1)} %collective-permute-done.23.refs_8_), channel_id=1, source_target_pairs={{0,8},{8,0},{1,9},{9,1},{2,10},{10,2},{3,11},{11,3},{4,12},{12,4},... | collective-permute-start | bytes 5160968 | tf_op jit(solution)/shard_map/ppermute | solution.py:549
  349.0 133.4 %collective-permute-start.27 = (bf16[1,224,1920]{2,1,0:T(8,128)(2,1)S(1)}, bf16[1,224,1920]{2,1,0:T(8,128)(2,1)}, u32[]{:S(2)}, u32[]{:S(2)}) collective-permute-start(bf16[1,224,1920]{2,1,0:T(8,128)(2,1)S(1)} %pad_maximum_fusion.8.refs_7_), channel_id=1, source_target_pairs={{0,8},{8,0},{1,9},{9,1},{2,10},{10,2},{3,11},{11,3},{4,12},{12,4},... | collective-permute-start | bytes 2580488 | tf_op jit(solution)/shard_map/ppermute | solution.py:549
  369.3 40.7 %collective-permute-start.21 = (bf16[2,224,1920]{2,1,0:T(8,128)(2,1)}, bf16[2,224,1920]{2,1,0:T(8,128)(2,1)}, u32[]{:S(2)}, u32[]{:S(2)}) collective-permute-start(bf16[2,224,1920]{2,1,0:T(8,128)(2,1)} %pad_maximum_fusion.2.refs_7_), channel_id=1, source_target_pairs={{0,8},{8,0},{1,9},{9,1},{2,10},{10,2},{3,11},{11,3},{4,12},{12,4},... | collective-permute-start | bytes 5160968 | tf_op jit(solution)/shard_map/ppermute | solution.py:549
  370.2 76.7 %collective-permute-start.22 = (bf16[2,224,1920]{2,1,0:T(8,128)(2,1)}, bf16[2,224,1920]{2,1,0:T(8,128)(2,1)}, u32[]{:S(2)}, u32[]{:S(2)}) collective-permute-start(bf16[2,224,1920]{2,1,0:T(8,128)(2,1)} %collective-permute-done.20.refs_8_), channel_id=1, source_target_pairs={{0,8},{8,0},{1,9},{9,1},{2,10},{10,2},{3,11},{11,3},{4,12},{12,4},... | collective-permute-start | bytes 5160968 | tf_op jit(solution)/shard_map/ppermute | solution.py:549
  371.4 115.1 %collective-permute-start.5 = (bf16[2112,896]{1,0:T(8,128)(2,1)}, bf16[2112,896]{1,0:T(8,128)(2,1)}, u32[]{:S(2)}, u32[]{:S(2)}) collective-permute-start(bf16[2112,896]{1,0:T(8,128)(2,1)} %collective-permute-done.1.refs_0_.refs_2_), channel_id=1, source_target_pairs={{0,2},{2,0},{1,3},{3,1},{4,6},{6,4},{5,7},{7,5},{8,10},{10,8},{9,1... | collective-permute-start | bytes 11354120 | tf_op jit(solution)/shard_map/ppermute | solution.py:549
  409.5 76.3 %collective-permute-start.17 = (bf16[2,224,1920]{2,1,0:T(8,128)(2,1)}, bf16[2,224,1920]{2,1,0:T(8,128)(2,1)}, u32[]{:S(2)}, u32[]{:S(2)}) collective-permute-start(bf16[2,224,1920]{2,1,0:T(8,128)(2,1)} %pad_maximum_fusion.1), channel_id=1, source_target_pairs={{0,4},{4,0},{1,5},{5,1},{2,6},{6,2},{3,7},{7,3},{8,12},{12,8},{9,1... | collective-permute-start | bytes 5160968 | tf_op jit(solution)/shard_map/ppermute | solution.py:549
  410.0 73.7 %collective-permute-start.7 = (bf16[1,224,1920]{2,1,0:T(8,128)(2,1)}, bf16[1,224,1920]{2,1,0:T(8,128)(2,1)}, u32[]{:S(2)}, u32[]{:S(2)}) collective-permute-start(bf16[1,224,1920]{2,1,0:T(8,128)(2,1)} %pad_maximum_fusion.7), channel_id=1, source_target_pairs={{0,4},{4,0},{1,5},{5,1},{2,6},{6,2},{3,7},{7,3},{8,12},{12,8},{9,1... | collective-permute-start | bytes 2580488 | tf_op jit(solution)/shard_map/ppermute | solution.py:549
  446.9 37.6 %collective-permute-start.28 = (bf16[1,224,1920]{2,1,0:T(8,128)(2,1)}, bf16[1,224,1920]{2,1,0:T(8,128)(2,1)}, u32[]{:S(2)}, u32[]{:S(2)}) collective-permute-start(bf16[1,224,1920]{2,1,0:T(8,128)(2,1)} %collective-permute-done.26.refs_8_), channel_id=1, source_target_pairs={{0,8},{8,0},{1,9},{9,1},{2,10},{10,2},{3,11},{11,3},{4,12},{12,4},... | collective-permute-start | bytes 2580488 | tf_op jit(solution)/shard_map/ppermute | solution.py:549
  482.4 102.2 %collective-permute-start.18 = (bf16[2,224,1920]{2,1,0:T(8,128)(2,1)}, bf16[2,224,1920]{2,1,0:T(8,128)(2,1)}, u32[]{:S(2)}, u32[]{:S(2)}) collective-permute-start(bf16[2,224,1920]{2,1,0:T(8,128)(2,1)} %pad_maximum_fusion.refs_7_), channel_id=1, source_target_pairs={{0,8},{8,0},{1,9},{9,1},{2,10},{10,2},{3,11},{11,3},{4,12},{12,4},... | collective-permute-start | bytes 5160968 | tf_op jit(solution)/shard_map/ppermute | solution.py:549
  483.7 55.8 %collective-permute-start.8 = (bf16[1,224,1920]{2,1,0:T(8,128)(2,1)S(1)}, bf16[1,224,1920]{2,1,0:T(8,128)(2,1)S(1)}, u32[]{:S(2)}, u32[]{:S(2)}) collective-permute-start(bf16[1,224,1920]{2,1,0:T(8,128)(2,1)S(1)} %copy-done.3), channel_id=1, source_target_pairs={{0,8},{8,0},{1,9},{9,1},{2,10},{10,2},{3,11},{11,3},{4,12},{12,4},... | collective-permute-start | bytes 2580488 | tf_op jit(solution)/shard_map/ppermute | solution.py:549
  484.5 73.6 %collective-permute-start.9 = (bf16[1,224,1920]{2,1,0:T(8,128)(2,1)}, bf16[1,224,1920]{2,1,0:T(8,128)(2,1)}, u32[]{:S(2)}, u32[]{:S(2)}) collective-permute-start(bf16[1,224,1920]{2,1,0:T(8,128)(2,1)} %collective-permute-done.7.refs_8_), channel_id=1, source_target_pairs={{0,8},{8,0},{1,9},{9,1},{2,10},{10,2},{3,11},{11,3},{4,12},{12,4},... | collective-permute-start | bytes 2580488 | tf_op jit(solution)/shard_map/ppermute | solution.py:549
  485.8 109.2 %collective-permute-start.19 = (bf16[2,224,1920]{2,1,0:T(8,128)(2,1)}, bf16[2,224,1920]{2,1,0:T(8,128)(2,1)}, u32[]{:S(2)}, u32[]{:S(2)}) collective-permute-start(bf16[2,224,1920]{2,1,0:T(8,128)(2,1)} %collective-permute-done.17.refs_8_), channel_id=1, source_target_pairs={{0,8},{8,0},{1,9},{9,1},{2,10},{10,2},{3,11},{11,3},{4,12},{12,4},... | collective-permute-start | bytes 5160968 | tf_op jit(solution)/shard_map/ppermute | solution.py:549
  486.5 173.8 %collective-permute-start.6 = (bf16[2112,896]{1,0:T(8,128)(2,1)}, bf16[2112,896]{1,0:T(8,128)(2,1)}, u32[]{:S(2)}, u32[]{:S(2)}) collective-permute-start(bf16[2112,896]{1,0:T(8,128)(2,1)} %collective-permute-done.5.refs_0_.refs_4_), channel_id=1, source_target_pairs={{0,1},{1,0},{2,3},{3,2},{4,5},{5,4},{6,7},{7,6},{8,9},{9,8},{10,11... | collective-permute-start | bytes 11354120 | tf_op jit(solution)/shard_map/ppermute | solution.py:549
  660.2 375.0 %collective-permute-start.33 = (f32[4,1040,896]{2,1,0:T(8,128)}, f32[4,1040,896]{2,1,0:T(8,128)}, u32[]{:S(2)}, u32[]{:S(2)}) collective-permute-start(f32[4,1040,896]{2,1,0:T(8,128)} %combine.14), channel_id=1, source_target_pairs={{0,1},{1,0},{2,3},{3,2},{4,5},{5,4},{6,7},{7,6},{8,9},{9,8},{10,11... | collective-permute-start | bytes 44728328 | tf_op jit(solution)/shard_map/ppermute | solution.py:549
  867.8 179.6 %collective-permute-start.29 = (f32[4,1040,896]{2,1,0:T(8,128)}, f32[4,1040,896]{2,1,0:T(8,128)}, u32[]{:S(2)}, u32[]{:S(2)}) collective-permute-start(f32[4,1040,896]{2,1,0:T(8,128)} %combine.10), channel_id=1, source_target_pairs={{0,1},{1,0},{2,3},{3,2},{4,5},{5,4},{6,7},{7,6},{8,9},{9,8},{10,11... | collective-permute-start | bytes 44728328 | tf_op jit(solution)/shard_map/ppermute | solution.py:549
  883.9 151.3 %collective-permute-start.41 = (f32[2,448,1920]{2,1,0:T(8,128)}, f32[2,448,1920]{2,1,0:T(8,128)}, u32[]{:S(2)}, u32[]{:S(2)}) collective-permute-start(f32[2,448,1920]{2,1,0:T(8,128)} %get-tuple-element.190), channel_id=1, source_target_pairs={{0,8},{8,0},{1,9},{9,1},{2,10},{10,2},{3,11},{11,3},{4,12},{12,4},... | collective-permute-start | bytes 20643848 | tf_op jit(solution)/shard_map/ppermute | solution.py:549
  883.9 298.8 %collective-permute-start.39 = (f32[2,448,1920]{2,1,0:T(8,128)}, f32[2,448,1920]{2,1,0:T(8,128)}, u32[]{:S(2)}, u32[]{:S(2)}) collective-permute-start(f32[2,448,1920]{2,1,0:T(8,128)} %get-tuple-element.188), channel_id=1, source_target_pairs={{0,8},{8,0},{1,9},{9,1},{2,10},{10,2},{3,11},{11,3},{4,12},{12,4},... | collective-permute-start | bytes 20643848 | tf_op jit(solution)/shard_map/ppermute | solution.py:549
  886.0 518.0 %collective-permute-start.43 = (f32[2,448,1920]{2,1,0:T(8,128)}, f32[2,448,1920]{2,1,0:T(8,128)}, u32[]{:S(2)}, u32[]{:S(2)}) collective-permute-start(f32[2,448,1920]{2,1,0:T(8,128)} %get-tuple-element.192), channel_id=1, source_target_pairs={{0,8},{8,0},{1,9},{9,1},{2,10},{10,2},{3,11},{11,3},{4,12},{12,4},... | collective-permute-start | bytes 20643848 | tf_op jit(solution)/shard_map/ppermute | solution.py:549
  1035.3 368.7 %collective-permute-start.45 = (f32[1,448,1920]{2,1,0:T(8,128)}, f32[1,448,1920]{2,1,0:T(8,128)}, u32[]{:S(2)}, u32[]{:S(2)}) collective-permute-start(f32[1,448,1920]{2,1,0:T(8,128)} %get-tuple-element.194), channel_id=1, source_target_pairs={{0,8},{8,0},{1,9},{9,1},{2,10},{10,2},{3,11},{11,3},{4,12},{12,4},... | collective-permute-start | bytes 10321928 | tf_op jit(solution)/shard_map/ppermute | solution.py:549
  1035.3 441.5 %collective-permute-start.37 = (f32[1,448,1920]{2,1,0:T(8,128)}, f32[1,448,1920]{2,1,0:T(8,128)}, u32[]{:S(2)}, u32[]{:S(2)}) collective-permute-start(f32[1,448,1920]{2,1,0:T(8,128)} %get-tuple-element.186), channel_id=1, source_target_pairs={{0,8},{8,0},{1,9},{9,1},{2,10},{10,2},{3,11},{11,3},{4,12},{12,4},... | collective-permute-start | bytes 10321928 | tf_op jit(solution)/shard_map/ppermute | solution.py:549
  1047.4 432.9 %collective-permute-start.35 = (f32[1040,896]{1,0:T(8,128)}, f32[1040,896]{1,0:T(8,128)}, u32[]{:S(2)}, u32[]{:S(2)}) collective-permute-start(f32[1040,896]{1,0:T(8,128)} %combine.16), channel_id=1, source_target_pairs={{0,2},{2,0},{1,3},{3,1},{4,6},{6,4},{5,7},{7,5},{8,10},{10,8},{9,1... | collective-permute-start | bytes 11182088 | tf_op jit(solution)/shard_map/ppermute | solution.py:549
  1182.7 480.5 %collective-permute-start.31 = (f32[1040,896]{1,0:T(8,128)}, f32[1040,896]{1,0:T(8,128)}, u32[]{:S(2)}, u32[]{:S(2)}) collective-permute-start(f32[1040,896]{1,0:T(8,128)} %combine.12), channel_id=1, source_target_pairs={{0,2},{2,0},{1,3},{3,1},{4,6},{6,4},{5,7},{7,5},{8,10},{10,8},{9,1... | collective-permute-start | bytes 11182088 | tf_op jit(solution)/shard_map/ppermute | solution.py:549
  1403.9 271.4 %collective-permute-start.40 = (f32[2,224,1920]{2,1,0:T(8,128)}, f32[2,224,1920]{2,1,0:T(8,128)}, u32[]{:S(2)}, u32[]{:S(2)}) collective-permute-start(f32[2,224,1920]{2,1,0:T(8,128)} %get-tuple-element.199), channel_id=1, source_target_pairs={{0,4},{4,0},{1,5},{5,1},{2,6},{6,2},{3,7},{7,3},{8,12},{12,8},{9,1... | collective-permute-start | bytes 10321928 | tf_op jit(solution)/shard_map/ppermute | solution.py:549
  1403.9 272.9 %collective-permute-start.42 = (f32[2,224,1920]{2,1,0:T(8,128)}, f32[2,224,1920]{2,1,0:T(8,128)}, u32[]{:S(2)}, u32[]{:S(2)}) collective-permute-start(f32[2,224,1920]{2,1,0:T(8,128)} %get-tuple-element.197), channel_id=1, source_target_pairs={{0,4},{4,0},{1,5},{5,1},{2,6},{6,2},{3,7},{7,3},{8,12},{12,8},{9,1... | collective-permute-start | bytes 10321928 | tf_op jit(solution)/shard_map/ppermute | solution.py:549
  1476.7 219.0 %collective-permute-start.44 = (f32[2,224,1920]{2,1,0:T(8,128)}, f32[2,224,1920]{2,1,0:T(8,128)}, u32[]{:S(2)}, u32[]{:S(2)}) collective-permute-start(f32[2,224,1920]{2,1,0:T(8,128)} %get-tuple-element.195), channel_id=1, source_target_pairs={{0,4},{4,0},{1,5},{5,1},{2,6},{6,2},{3,7},{7,3},{8,12},{12,8},{9,1... | collective-permute-start | bytes 10321928 | tf_op jit(solution)/shard_map/ppermute | solution.py:549
  1480.3 182.9 %collective-permute-start.38 = (f32[1,224,1920]{2,1,0:T(8,128)}, f32[1,224,1920]{2,1,0:T(8,128)}, u32[]{:S(2)}, u32[]{:S(2)}) collective-permute-start(f32[1,224,1920]{2,1,0:T(8,128)} %get-tuple-element.203), channel_id=1, source_target_pairs={{0,4},{4,0},{1,5},{5,1},{2,6},{6,2},{3,7},{7,3},{8,12},{12,8},{9,1... | collective-permute-start | bytes 5160968 | tf_op jit(solution)/shard_map/ppermute | solution.py:549
  1663.2 198.1 %collective-permute-start.34 = (f32[1040,896]{1,0:T(8,128)}, f32[1040,896]{1,0:T(8,128)}, u32[]{:S(2)}, u32[]{:S(2)}) collective-permute-start(f32[1040,896]{1,0:T(8,128)} %combine.15), channel_id=1, source_target_pairs={{0,2},{2,0},{1,3},{3,1},{4,6},{6,4},{5,7},{7,5},{8,10},{10,8},{9,1... | collective-permute-start | bytes 11182088 | tf_op jit(solution)/shard_map/ppermute | solution.py:549
  1663.2 198.1 %collective-permute-start.36 = (f32[1040,896]{1,0:T(8,128)}, f32[1040,896]{1,0:T(8,128)}, u32[]{:S(2)}, u32[]{:S(2)}) collective-permute-start(f32[1040,896]{1,0:T(8,128)} %combine.17), channel_id=1, source_target_pairs={{0,4},{4,0},{1,5},{5,1},{2,6},{6,2},{3,7},{7,3},{8,12},{12,8},{9,1... | collective-permute-start | bytes 11182088 | tf_op jit(solution)/shard_map/ppermute | solution.py:549
  1675.3 197.2 %collective-permute-start.30 = (f32[1040,896]{1,0:T(8,128)}, f32[1040,896]{1,0:T(8,128)}, u32[]{:S(2)}, u32[]{:S(2)}) collective-permute-start(f32[1040,896]{1,0:T(8,128)} %combine.11), channel_id=1, source_target_pairs={{0,2},{2,0},{1,3},{3,1},{4,6},{6,4},{5,7},{7,5},{8,10},{10,8},{9,1... | collective-permute-start | bytes 11182088 | tf_op jit(solution)/shard_map/ppermute | solution.py:549
  1676.8 195.7 %collective-permute-start.32 = (f32[1040,896]{1,0:T(8,128)}, f32[1040,896]{1,0:T(8,128)}, u32[]{:S(2)}, u32[]{:S(2)}) collective-permute-start(f32[1040,896]{1,0:T(8,128)} %combine.13), channel_id=1, source_target_pairs={{0,4},{4,0},{1,5},{5,1},{2,6},{6,2},{3,7},{7,3},{8,12},{12,8},{9,1... | collective-permute-start | bytes 11182088 | tf_op jit(solution)/shard_map/ppermute | solution.py:549
  1695.8 164.2 %collective-permute-start.46 = (f32[1,224,1920]{2,1,0:T(8,128)S(1)}, f32[1,224,1920]{2,1,0:T(8,128)S(1)}, u32[]{:S(2)}, u32[]{:S(2)}) collective-permute-start(f32[1,224,1920]{2,1,0:T(8,128)S(1)} %get-tuple-element.201), channel_id=1, source_target_pairs={{0,4},{4,0},{1,5},{5,1},{2,6},{6,2},{3,7},{7,3},{8,12},{12,8},{9,1... | collective-permute-start | bytes 5160968 | tf_op jit(solution)/shard_map/ppermute | solution.py:549
  (14 other events, 935.1 us)
